TPU v7x, 128 devices: a whole 4x4x4 slice. The times are simulated.
128 devices in a mesh: dp: 8 (over z_hi, x), expert: 16 (over y, z_lo, core).
Axes of the slice: x: 4, y: 4, z: 4 (z_hi: 2, z_lo: 2; z = z_hi * 2 + z_lo), core: 2. Of those that a mesh axis runs over, the one named last changes fastest.
Arguments:
- tokens: bfloat16 [32768, 2048], P(('dp', 'expert')), may hold values from -6 to 6
- expert_ids: int32 [32768, 8], P(('dp', 'expert')), may hold values from 0 to 31, all different within a row; in each aligned block of 256 rows (0 to 255, 256 to 511, ...) at most 80 rows name the same one
- route_probs: float32 [32768, 8], P(('dp', 'expert')), may hold values from 0.05 to 1
- w_gate_up: bfloat16 [32, 2048, 1536], P('expert', 'dp'), may hold values from -0.125 to 0.125
- w_down: bfloat16 [32, 768, 2048], P('expert', None, 'dp'), may hold values from -0.21875 to 0.21875
Outputs:
- moe_out: bfloat16 [32768, 2048], P(('dp', 'expert'))
Inputs may be any that keep to these rules, and one draw needn't show every extreme that they name: `expert_ids`: each row names 8 different experts. Among the rows of one device no expert is named more than 80 times, and in every draw some expert is named exactly 80 times in some device's rows.
All inputs are finite; a program needn't handle non-finite values.
Results may differ from a plain program's by a relative error of at most 0.0057.
Values may be sent and summed in bfloat16 or wider, within the bound.
A program may use at most 128 MiB of HBM per device.

v0:
```python
import jax
import jax.numpy as jnp
from jax import lax
from jax.sharding import Mesh
from jax.sharding import PartitionSpec as P

DP = ("dp_0", "dp_1")
DP_EXPERT = ("dp_0", "dp_1", "expert")


def joined_along(pieces, dim):
    pieces = jnp.moveaxis(pieces, 0, dim)
    shape = pieces.shape
    return pieces.reshape(*shape[:dim], shape[dim] * shape[dim + 1], *shape[dim + 2 :])


def gather_in_order(array, axes, sequence):
    pieces = array
    for k in sequence:
        pieces = lax.all_gather(pieces, axes[k])
    done = sequence[::-1]
    back = [done.index(k) for k in range(len(axes))]
    pieces = pieces.transpose(*back, *range(len(axes), pieces.ndim))
    return pieces.reshape(-1, *array.shape)


def whole_of(array, axes, sequence, dim):
    return joined_along(gather_in_order(array, axes, sequence), dim)


def shards(tokens, expert_ids, route_probs, w_gate_up, w_down):
    owners = lax.axis_size("expert")
    local_count = w_gate_up.shape[0]
    experts = owners * local_count
    tok_rows = tokens.shape[0]
    model_width = tokens.shape[1]
    top_count = expert_ids.shape[1]
    capacity = 5 * tok_rows * top_count // (4 * experts)
    hidden_units = w_down.shape[1]
    flat_ids = expert_ids.reshape(-1)
    onehot = (flat_ids[:, None] == jnp.arange(experts, dtype=jnp.int32)[None, :]).astype(jnp.int32)
    before = jnp.cumsum(onehot, axis=0) - onehot
    slot_of = jnp.sum(before * onehot, axis=1)
    target = flat_ids * capacity + slot_of
    copies = jnp.repeat(tokens, top_count, axis=0)
    send_buffer = jnp.zeros((experts * capacity, model_width), jnp.bfloat16).at[target].set(copies)
    send_buffer = send_buffer.reshape(experts, capacity, model_width)
    received = lax.all_to_all(send_buffer, "expert", split_axis=0, concat_axis=1, tiled=True)
    returned_list = []
    for local_expert in range(local_count):
        rows_in = received[local_expert]
        joined = jnp.dot(
            rows_in,
            whole_of(w_gate_up[local_expert], DP, (0, 1), 0),
            preferred_element_type=jnp.float32,
        )
        hidden = (jax.nn.silu(joined[:, :hidden_units]) * joined[:, hidden_units:]).astype(
            jnp.bfloat16
        )
        returned_list.append(
            lax.all_to_all(
                jnp.dot(
                    hidden,
                    lax.all_gather(w_down[local_expert], DP, axis=1, tiled=True),
                    preferred_element_type=jnp.float32,
                ).astype(jnp.bfloat16),
                "expert",
                split_axis=0,
                concat_axis=0,
                tiled=True,
            )
        )
    returned = jnp.concatenate(returned_list, axis=0)
    source_rows = (
        flat_ids % local_count * (owners * capacity) + flat_ids // local_count * capacity + slot_of
    )
    gathered = returned[source_rows].reshape(tok_rows, top_count, model_width)
    weights = route_probs / jnp.sum(route_probs, axis=1, keepdims=True)
    combined = jnp.sum(gathered.astype(jnp.float32) * weights[:, :, None], axis=1)
    return combined.astype(jnp.bfloat16)


def solution(mesh):
    finer = Mesh(mesh.devices.reshape(2, 4, mesh.shape["expert"]), ("dp_0", "dp_1", "expert"))
    in_specs = (
        P(DP_EXPERT, None),
        P(DP_EXPERT, None),
        P(DP_EXPERT, None),
        P("expert", DP, None),
        P("expert", None, DP),
    )
    out_specs = P(DP_EXPERT, None)
    return jax.shard_map(
        shards, mesh=finer, in_specs=in_specs, out_specs=out_specs, check_vma=False
    )
```

profile of v0, /device:TPU:49, one launch (start us, length us, event | category | flops | bytes accessed | tf_op | source)
XLA Modules:
  0.0 568.5 jit_solution(15967926868259111235)
XLA Ops:
  6.5 0.0 copy-start
  6.5 0.0 copy-start.3
  6.5 0.0 copy-start.5
  6.5 0.0 all-gather.11.cloned.1.call-start
  6.5 2.8 fusion.23
  9.3 0.0 all-gather.11.cloned.1.call-update
  9.3 0.0 all-gather.13.cloned.1.call-start
  9.4 0.7 all-gather.13.cloned.1.call-update
  10.1 0.0 all-gather.15.cloned.1.call-start
  10.1 31.5 %all-gather.11.cloned.1.call-done = bf16[2,256,1536]{2,1,0:T(8,128)(2,1)} async-done(((bf16[1,256,1536]{2,1,0:T(8,128)(2,1)}), bf16[2,256,1536]{2,1,0:T(8,128)(2,1)}) %all-gather.11.cloned.1.call-update) | async-done | bytes 1572880 | tf_op jit(solution)/shard_map/all_gather | solution.py:20
  41.6 0.0 all-gather.15.cloned.1.call-update
  41.6 0.0 all-gather.17.cloned.1.call-start
  41.7 0.0 copy-done.3
  41.7 1.0 fusion.24
  42.7 0.0 all-gather.17.cloned.1.call-update
  42.7 0.0 copy-done.5
  42.7 0.1 copy.21
  42.8 0.1 eq.31
  42.9 0.1 eq.27
  43.0 0.1 reshape.185
  43.2 9.1 %reduce-window.6 = s32[32,16,128]{2,1,0:T(8,128)S(1)} reduce-window(s32[32,16,128]{2,1,0:T(8,128)S(1)} %fusion.16, s32[]{:T(128)} %constant.38.clone.1), window={size=1x1x128 pad=0_0x0_0x127_0}, to_apply=%region_0.0 | reduce-window | flops 8323072 | bytes 524292 | tf_op jit(solution)/shard_map/reduce-window
  52.3 0.1 slice.52
  52.4 0.2 copy.29
  52.7 0.2 reduce-window.9
  52.8 0.1 broadcast_add_fusion
  53.0 0.1 fusion.15
  53.1 0.1 compare_select_fusion
  53.2 0.0 copy-done
  53.2 17.9 %scatter_custom_fusion = bf16[2560,2048]{1,0:T(8,128)(2,1)} fusion(s32[2048]{0:T(1024)S(1)} %bitcast.73, bf16[]{:T(256)} %constant.36.clone.1, bf16[256,2048]{1,0:T(8,128)(2,1)S(1)} %copy-done), kind=kCustom, calls=%fused_computation.5 | custom fusion | bytes 11534338 | tf_op jit(solution)/shard_map/scatter | solution.py:46
  71.1 6.4 %all-to-all-start = ((bf16[32,80,2048]{2,1,0:T(8,128)(2,1)}), bf16[32,80,2048]{2,1,0:T(8,128)(2,1)}, u32[]{:S(2)}, u32[]{:S(2)}) async-start(bf16[32,80,2048]{2,1,0:T(8,128)(2,1)} %bitcast.57), calls=%async_computation | async-start | bytes 20971520 | tf_op jit(solution)/shard_map/all_to_all | solution.py:48
  77.5 0.0 all-gather.19.cloned.1.call-start
  77.6 0.0 all-gather.13.cloned.1.call-done
  77.6 0.5 all-gather.19.cloned.1.call-update
  78.1 0.2 all-gather.21.cloned.1.call-start
  78.3 0.4 all-gather.21.cloned.1.call-update
  78.7 165.6 %all-to-all-done = bf16[32,80,2048]{2,1,0:T(8,128)(2,1)} async-done(((bf16[32,80,2048]{2,1,0:T(8,128)(2,1)}), bf16[32,80,2048]{2,1,0:T(8,128)(2,1)}, u32[]{:S(2)}, u32[]{:S(2)}) %all-to-all-start) | async-done | bytes 10485792 | tf_op jit(solution)/shard_map/all_to_all | solution.py:48
  244.3 10.1 %fusion.22 = (bf16[1,16,80,2048]{3,2,0,1:T(8,128)(2,1)}, bf16[1,16,80,2048]{3,2,0,1:T(8,128)(2,1)}) fusion(bf16[2,16,80,2048]{3,2,0,1:T(8,128)(2,1)} %bitcast.8), kind=kLoop, calls=%fused_computation.41 | loop fusion | bytes 20971520 | tf_op jit(solution)/shard_map/slice | solution.py:51
  254.4 0.0 all-gather.15.cloned.1.call-done
  254.4 0.0 copy-start.2
  254.4 3.6 copy.26
  258.0 0.7 copy-done.2
  258.7 10.6 %fusion.25 = f32[1280,1536]{1,0:T(8,128)} fusion(bf16[1280,2048]{1,0:T(8,128)(2,1)S(1)} %bitcast.65, bf16[2048,1536]{1,0:T(8,128)(2,1)S(1)} %bitcast.61), kind=kOutput, calls=%fused_computation.44 | convolution fusion | flops 8053063680 | bytes 19398656 | tf_op jit(solution)/shard_map/dot_general | solution.py:52
  269.3 0.0 all-gather.17.cloned.1.call-done
  269.3 10.9 %convolution_convert_fusion.1 = bf16[1280,2048]{1,0:T(8,128)(2,1)} fusion(bf16[1,768,2048]{2,1,0:T(8,128)(2,1)} %all-gather.17.cloned.1.call-done, f32[1280,1536]{1,0:T(8,128)} %fusion.25), kind=kOutput, calls=%fused_computation.8 | convolution fusion | flops 4035051520 | bytes 16252928 | tf_op jit(solution)/shard_map/dot_general | solution.py:62
  280.2 0.0 slice-start
  280.2 9.1 %all-to-all-start.1 = ((bf16[16,80,2048]{2,1,0:T(8,128)(2,1)}), bf16[16,80,2048]{2,1,0:T(8,128)(2,1)}, u32[]{:S(2)}, u32[]{:S(2)}) async-start(bf16[16,80,2048]{2,1,0:T(8,128)(2,1)} %bitcast.66), calls=%async_computation.1 | async-start | bytes 10485760 | tf_op jit(solution)/shard_map/all_to_all | solution.py:61
  289.3 48.6 %all-gather.19.cloned.1.call-done = bf16[8,256,1536]{2,1,0:T(8,128)(2,1)} async-done(((bf16[2,256,1536]{2,1,0:T(8,128)(2,1)}), bf16[8,256,1536]{2,1,0:T(8,128)(2,1)}) %all-gather.19.cloned.1.call-update) | async-done | bytes 6291472 | tf_op jit(solution)/shard_map/all_gather | solution.py:20
  337.9 0.0 slice-start.1
  337.9 3.6 copy.27
  341.5 0.0 slice-done
  341.6 0.4 slice-done.1
  341.9 10.5 %fusion.26 = f32[1280,1536]{1,0:T(8,128)} fusion(bf16[1280,2048]{1,0:T(8,128)(2,1)S(1)} %bitcast.64, bf16[2048,1536]{1,0:T(8,128)(2,1)S(1)} %bitcast.60), kind=kOutput, calls=%fused_computation.45 | convolution fusion | flops 8053063680 | bytes 19398656 | tf_op jit(solution)/shard_map/dot_general | solution.py:52
  352.5 63.8 %all-gather.21.cloned.1.call-done = bf16[1,768,2048]{2,1,0:T(8,128)(2,1)} async-done(((bf16[1,768,256]{2,1,0:T(8,128)(2,1)}), bf16[1,768,2048]{2,1,0:T(8,128)(2,1)}) %all-gather.21.cloned.1.call-update) | async-done | bytes 3145744 | tf_op jit(solution)/shard_map/all_gather | solution.py:64
  416.3 10.8 %convolution_convert_fusion = bf16[1280,2048]{1,0:T(8,128)(2,1)} fusion(bf16[1,768,2048]{2,1,0:T(8,128)(2,1)} %all-gather.21.cloned.1.call-done, f32[1280,1536]{1,0:T(8,128)} %fusion.26), kind=kOutput, calls=%fused_computation.7 | convolution fusion | flops 4035051520 | bytes 16252928 | tf_op jit(solution)/shard_map/dot_general | solution.py:62
  427.1 0.0 all-to-all-done.1
  427.1 0.0 copy-start.4
  427.1 7.5 %all-to-all-start.2 = ((bf16[16,80,2048]{2,1,0:T(8,128)(2,1)}), bf16[16,80,2048]{2,1,0:T(8,128)(2,1)}, u32[]{:S(2)}, u32[]{:S(2)}) async-start(bf16[16,80,2048]{2,1,0:T(8,128)(2,1)} %bitcast.67), calls=%async_computation.2 | async-start | bytes 10485760 | tf_op jit(solution)/shard_map/all_to_all | solution.py:61
  434.6 0.0 copy-done.4
  434.6 0.1 copy.28
  434.8 79.5 %all-to-all-done.2 = bf16[16,80,2048]{2,1,0:T(8,128)(2,1)} async-done(((bf16[16,80,2048]{2,1,0:T(8,128)(2,1)}), bf16[16,80,2048]{2,1,0:T(8,128)(2,1)}, u32[]{:S(2)}, u32[]{:S(2)}) %all-to-all-start.2) | async-done | bytes 5242912 | tf_op jit(solution)/shard_map/all_to_all | solution.py:61
  514.3 12.7 %pad_maximum_fusion = bf16[2560,2048]{1,0:T(8,128)(2,1)} fusion(bf16[1280,2048]{1,0:T(8,128)(2,1)} %bitcast.23, bf16[1280,2048]{1,0:T(8,128)(2,1)} %bitcast.15), kind=kLoop, calls=%fused_computation.4 | loop fusion | flops 20971520 | bytes 20971520 | tf_op jit(solution)/shard_map/concatenate | solution.py:73
  527.0 22.0 %gather_fusion = bf16[2048,2048]{1,0:T(8,128)(2,1)} fusion(bf16[2560,2048]{1,0:T(8,128)(2,1)} %pad_maximum_fusion, s32[2048]{0:T(1024)S(1)} %broadcast_clamp_fusion), kind=kCustom, calls=%fused_computation | custom fusion | bytes 16785408 | tf_op jit(solution)/shard_map/gather | solution.py:77
  549.0 12.2 %fusion = bf16[256,2048]{1,0:T(8,128)(2,1)} fusion(bf16[2048,2048]{1,0:T(8,128)(2,1)} %gather_fusion, f32[256,8]{1,0:T(8,128)S(1)} %copy.28), kind=kLoop, calls=%fused_computation.3 | loop fusion | flops 12058624 | bytes 9445376 | tf_op jit(solution)/shard_map/reduce_sum | solution.py:79
  561.2 0.0 copy-done.1
  (6 shorter events, 0.1 us)
Async XLA Ops:
  6.5 46.7 %copy-start = (bf16[256,2048]{1,0:T(8,128)(2,1)S(1)}, bf16[256,2048]{1,0:T(8,128)(2,1)}, u32[]{:S(2)}) copy-start(bf16[256,2048]{1,0:T(8,128)(2,1)} %param.5) | copy-start | bytes 3145732
  6.5 35.2 %copy-start.3 = (bf16[2,768,256]{2,1,0:T(8,128)(2,1)S(1)}, bf16[2,768,256]{2,1,0:T(8,128)(2,1)}, u32[]{:S(2)}) copy-start(bf16[2,768,256]{2,1,0:T(8,128)(2,1)} %param.9) | copy-start | bytes 2359300
  6.5 36.1 %copy-start.5 = (s32[256,8]{0,1:T(8,128)S(1)}, s32[256,8]{0,1:T(8,128)}, u32[]{:S(2)}) copy-start(s32[256,8]{0,1:T(8,128)} %param.6) | copy-start | bytes 24580
  6.5 35.1 %all-gather.11.cloned.1.call-start = ((), (), s32[]{:S(2)}) async-start(), calls=%async_computation.3 | async-start | bytes 2359296 | tf_op jit(solution)/shard_map/all_gather | solution.py:20
  9.3 68.3 %all-gather.13.cloned.1.call-start = ((), (), s32[]{:S(2)}) async-start(), calls=%async_computation.4 | async-start | bytes 2359296 | tf_op jit(solution)/shard_map/all_gather | solution.py:20
  10.1 244.3 %all-gather.15.cloned.1.call-start = ((), (), s32[]{:S(2)}) async-start(), calls=%async_computation.5 | async-start | bytes 7864320 | tf_op jit(solution)/shard_map/all_gather | solution.py:20
  41.6 227.6 %all-gather.17.cloned.1.call-start = ((), (), s32[]{:S(2)}) async-start(), calls=%async_computation.6 | async-start | bytes 3538944 | tf_op jit(solution)/shard_map/all_gather | solution.py:64
  71.1 173.2 %all-to-all-start = ((bf16[32,80,2048]{2,1,0:T(8,128)(2,1)}), bf16[32,80,2048]{2,1,0:T(8,128)(2,1)}, u32[]{:S(2)}, u32[]{:S(2)}) async-start(bf16[32,80,2048]{2,1,0:T(8,128)(2,1)} %bitcast.57), calls=%async_computation | async-start | bytes 20971520 | tf_op jit(solution)/shard_map/all_to_all | solution.py:48
  77.5 260.4 %all-gather.19.cloned.1.call-start = ((), (), s32[]{:S(2)}) async-start(), calls=%async_computation.7 | async-start | bytes 7864320 | tf_op jit(solution)/shard_map/all_gather | solution.py:20
  78.1 338.2 %all-gather.21.cloned.1.call-start = ((), (), s32[]{:S(2)}) async-start(), calls=%async_computation.8 | async-start | bytes 3538944 | tf_op jit(solution)/shard_map/all_gather | solution.py:64
  254.4 4.3 copy-start.2
  280.2 61.3 %slice-start = ((s8[5242880]{0:T(1024)(128)(4,1)}), s8[1048576]{0:T(1024)(128)(4,1)S(1)}, s32[]{:S(2)}) async-start(s8[5242880]{0:T(1024)(128)(4,1)} %bitcast.62), calls=%async_computation.9 | async-start | bytes 2097152
  280.2 146.9 %all-to-all-start.1 = ((bf16[16,80,2048]{2,1,0:T(8,128)(2,1)}), bf16[16,80,2048]{2,1,0:T(8,128)(2,1)}, u32[]{:S(2)}, u32[]{:S(2)}) async-start(bf16[16,80,2048]{2,1,0:T(8,128)(2,1)} %bitcast.66), calls=%async_computation.1 | async-start | bytes 10485760 | tf_op jit(solution)/shard_map/all_to_all | solution.py:61
  337.9 4.0 slice-start.1
  427.1 7.5 %copy-start.4 = (f32[256,8]{0,1:T(8,128)S(1)}, f32[256,8]{0,1:T(8,128)}, u32[]{:S(2)}) copy-start(f32[256,8]{0,1:T(8,128)} %param.7) | copy-start | bytes 24580
  427.1 87.2 %all-to-all-start.2 = ((bf16[16,80,2048]{2,1,0:T(8,128)(2,1)}), bf16[16,80,2048]{2,1,0:T(8,128)(2,1)}, u32[]{:S(2)}, u32[]{:S(2)}) async-start(bf16[16,80,2048]{2,1,0:T(8,128)(2,1)} %bitcast.67), calls=%async_computation.2 | async-start | bytes 10485760 | tf_op jit(solution)/shard_map/all_to_all | solution.py:61
  527.0 34.2 %copy-start.1 = (bf16[256,2048]{1,0:T(8,128)(2,1)S(1)}, bf16[256,2048]{1,0:T(8,128)(2,1)}, u32[]{:S(2)}) copy-start(bf16[256,2048]{1,0:T(8,128)(2,1)} %param.5) | copy-start | bytes 3145732
Sparse Core Ops, SparseCore 0:
  9.4 32.1 all-gather.10
  43.3 30.5 all-gather.12
  75.5 65.7 all-gather.14
  143.3 99.1 all-gather.16
  244.0 93.8 all-gather.18
  340.0 76.2 all-gather.20
where the time goes:
time: 576 us; the launch traced here: 569 us
  waiting for transfers between devices  391 us (68%)
  local copies, waits for them, and re-layouts  62.9 us (11%)
  matrix products  42.8 us (7%)
  other arithmetic  34.6 us (6%)
  starting transfers between devices  23.4 us (4%)
  between operations  14.1 us (2%)
    all_to_all x1, waiting for transfers between devices, shards(): lax.all_to_all(send_buffer, 'expert', split_axis=0, concat_axis=1, tiled=...  166 us
    all_gather x4, waiting for transfers between devices, gather_in_order(): pieces = lax.all_gather(pieces, axes[k])  80.1 us
    all_to_all x2, waiting for transfers between devices, shards(): lax.all_to_all(jnp.dot(hidden, lax.all_gather(w_down[local_expert], DP, a...  79.5 us
    all_gather x2, waiting for transfers between devices, shards(): lax.all_gather(w_down[local_expert], DP, axis=1, tiled=True)  63.8 us
    gather x1, local copies, waits for them, and re-layouts, shards(): gathered = returned[source_rows].reshape(tok_rows, top_count, model_width)  22 us
    dot_general x2, matrix products, shards(): jnp.dot(hidden, lax.all_gather(w_down[local_expert], DP, axis=1, tiled=Tr...  21.7 us
    dot_general x2, matrix products, shards(): jnp.dot(rows_in, whole_of(w_gate_up[local_expert], DP, (0, 1), 0), prefer...  21.1 us
    scatter x1, local copies, waits for them, and re-layouts, shards(): jnp.zeros((experts * capacity, model_width), jnp.bfloat16).at[target]  17.9 us
  transfers between devices with their start and end apart: 9, of which 5 were waited for; matrix products, arithmetic and copies ran while one was open for 16% of the time, Pallas kernels for 0%

commit v1 on v0

v1 whole, which is shorter than its diff:
```python
import jax
import jax.numpy as jnp
from jax import lax
from jax.experimental import pallas as pl
from jax.experimental.pallas import tpu as pltpu
from jax.sharding import PartitionSpec as P

MESH = pl.DeviceIdType.MESH
F32 = jnp.float32
BF16 = jnp.bfloat16

TOK = 256
META = 16
ROWS = TOK + META
HALF = 144
D = 2048
FF = 768
TOP = 8
CAP = 80
SRC = 16
COL = 256
STEPS = 8
MOVES = 17 + 4 * 9 + 2 * 8 + 2 * 9

OWN, ZED, LEFT, RIGHT, ACROSS, ZLEFT, ZRIGHT, ZACROSS = range(0, 16, 2)
RETURN = {
    (0, 0): OWN, (0, 1): ZED, (1, 0): RIGHT, (1, 1): ZRIGHT,
    (2, 0): ACROSS, (2, 1): ZACROSS, (3, 0): LEFT, (3, 1): ZLEFT,
}
PIECES = [(e, n) for e in range(2) for n in range(3)]
Z_FIRST = (0, 1, 2, 3)
X_FIRST = (4, 5)


def kernel(
    tok, ids, probs, wgu, wdn, out,
    tokb, wg, wd, xs, hid, pt, yb, tri, zbuf,
    local_sem, send_sem, recv_sem, ret_send, ret_recv, free_sem,
):
    dp, ex = lax.axis_index("dp"), lax.axis_index("expert")
    zh, x = dp // 4, dp % 4
    y, zl, core = ex // 4, (ex // 2) % 2, ex % 2
    xl, xr, xa = (x + 3) % 4, (x + 1) % 4, (x + 2) % 4

    def at_dp(zhi, xx):
        return (zhi * 4 + xx, ex)

    def at_ex(yy, zz, cc):
        return (dp, (yy * 2 + zz) * 2 + cc)

    x_right, x_left, z_far = at_dp(zh, xr), at_dp(zh, xl), at_dp(1 - zh, x)
    y_right, y_left = at_ex((y + 1) % 4, zl, core), at_ex((y + 3) % 4, zl, core)
    z_near, twin = at_ex(y, 1 - zl, core), at_ex(y, zl, 1 - core)

    count = [0]

    class Move:
        def __init__(self, src, dst, device, lands=None):
            n = count[0]
            count[0] += 1
            sems = dict(send_sem=send_sem.at[n], recv_sem=recv_sem.at[n], device_id=device, device_id_type=MESH)
            lands = dst if lands is None else lands
            self.out = lambda: pltpu.make_async_remote_copy(src_ref=src, dst_ref=dst, **sems)
            self.into = lambda: pltpu.make_async_remote_copy(src_ref=lands, dst_ref=lands, **sems)

        def start(self):
            self.out().start()

        def wait_send(self):
            self.out().wait_send()

        def wait_recv(self):
            self.into().wait_recv()

    def start(*moves):
        for m in moves:
            m.start()

    def wait(*moves):
        for m in moves:
            m.wait_recv()

    first, second = pl.ds(0, HALF), pl.ds(HALF, ROWS - HALF)

    def block(src, dst, device, rows=None):
        if rows is None:
            return Move(tokb.at[src], tokb.at[dst], device)
        return Move(tokb.at[src, rows], tokb.at[dst, rows], device)

    t_z = block(OWN, ZED, z_near)
    t_right, t_left = block(OWN, LEFT, y_right), block(OWN, RIGHT, y_left)
    t_fwd_r, t_fwd_l = block(LEFT, ACROSS, y_right, first), block(RIGHT, ACROSS, y_left, second)
    t_zright, t_zleft = block(ZED, ZLEFT, y_right), block(ZED, ZRIGHT, y_left)
    t_zfwd_r, t_zfwd_l = block(ZLEFT, ZACROSS, y_right, first), block(ZRIGHT, ZACROSS, y_left, second)
    twins = {s: block(s, s + 1, twin) for s in range(0, SRC, 2)}
    token_moves = [t_z, t_right, t_left, t_fwd_r, t_fwd_l, t_zright, t_zleft, t_zfwd_r, t_zfwd_l, *twins.values()]

    def gate_up_moves(e, n, x_first):
        def move(device, sends, takes, rows=None):
            src, lands = wg.at[e, n, sends[0] * 4 + sends[1]], wg.at[e, n, takes[0] * 4 + takes[1]]
            if rows is not None:
                src, lands = src.at[rows], lands.at[rows]
            return Move(src, src, device, lands)

        top, low = pl.ds(0, COL // 2), pl.ds(COL // 2, COL // 2)
        far = 1 - zh
        moves = dict(
            right=move(x_right, (zh, x), (zh, xl)), left=move(x_left, (zh, x), (zh, xr)),
            fwd_r=move(x_right, (zh, xl), (zh, xa), top), fwd_l=move(x_left, (zh, xr), (zh, xa), low),
            z=move(z_far, (zh, x), (far, x)),
        )
        if x_first:
            moves.update(
                zl=move(z_far, (zh, xl), (far, xl)), zr=move(z_far, (zh, xr), (far, xr)),
                za=move(z_far, (zh, xa), (far, xa)),
            )
        else:
            moves.update(
                zright=move(x_right, (far, x), (far, xl)), zleft=move(x_left, (far, x), (far, xr)),
                zfwd_r=move(x_right, (far, xl), (far, xa), top), zfwd_l=move(x_left, (far, xr), (far, xa), low),
            )
        return moves

    def down_moves(e):
        top, low = pl.ds(0, FF // 2), pl.ds(FF // 2, FF // 2)

        def move(device, src, dst, rows=None):
            if rows is None:
                return Move(wd.at[e, src], wd.at[e, dst], device)
            return Move(wd.at[e, src, rows], wd.at[e, dst, rows], device)

        return dict(
            right=move(x_right, 0, 1), left=move(x_left, 0, 3), z=move(z_far, 0, 4),
            fwd_r=move(x_right, 1, 2, top), fwd_l=move(x_left, 3, 2, low),
            zright=move(x_right, 4, 5), zleft=move(x_left, 4, 7),
            zfwd_r=move(x_right, 5, 6, top), zfwd_l=move(x_left, 7, 6, low),
        )

    gu = [gate_up_moves(e, n, p in X_FIRST) for p, (e, n) in enumerate(PIECES)]
    dn = [down_moves(0), down_moves(1)]

    mine = zh * 4 + x
    loads = {}

    def load(name, src, dst):
        loads[name] = pltpu.make_async_copy(src, dst, local_sem.at[len(loads)])
        loads[name].start()

    order = X_FIRST + Z_FIRST
    for p in order[:2]:
        e, n = PIECES[p]
        load((p, 0), wgu.at[e, :, pl.ds(n * COL, COL)], wg.at[e, n, mine, :, pl.ds(0, COL)])
        load((p, 1), wgu.at[e, :, pl.ds(FF + n * COL, COL)], wg.at[e, n, mine, :, pl.ds(COL, COL)])
    load("tok", tok, tokb.at[OWN, pl.ds(0, TOK)])
    for p in order[2:]:
        e, n = PIECES[p]
        load((p, 0), wgu.at[e, :, pl.ds(n * COL, COL)], wg.at[e, n, mine, :, pl.ds(0, COL)])
        load((p, 1), wgu.at[e, :, pl.ds(FF + n * COL, COL)], wg.at[e, n, mine, :, pl.ds(COL, COL)])
    load("down0", wdn.at[0], wd.at[0, 0])
    load("down1", wdn.at[1], wd.at[1, 0])

    barrier = pltpu.get_barrier_semaphore()
    for peer in (x_right, x_left, z_far, y_right, y_left, z_near, twin):
        pl.semaphore_signal(barrier, inc=1, device_id=peer, device_id_type=MESH)

    weights = probs[...] / jnp.sum(probs[...], axis=0, keepdims=True)
    high = weights.astype(BF16)
    middle = (weights - high.astype(F32)).astype(BF16)
    low = (weights - high.astype(F32) - middle.astype(F32)).astype(BF16)
    numbers = ids[...].astype(F32).astype(BF16)
    for k in range(TOP):
        parts = [v[k : k + 1, :] for v in (numbers, high, middle, low)]
        rows = jnp.concatenate([*parts, jnp.zeros((META - 4, TOK), BF16)], axis=0)
        tokb[OWN, TOK:ROWS, k * TOK : (k + 1) * TOK] = rows

    before = lax.broadcasted_iota(jnp.int32, (TOK, TOK), 0)
    after = lax.broadcasted_iota(jnp.int32, (TOK, TOK), 1)
    tri[...] = jnp.where(before < after, 1.0, 0.0).astype(BF16)
    pl.semaphore_wait(barrier, 7)

    slot_number = lax.broadcasted_iota(jnp.int32, (CAP, TOK), 0).astype(F32)

    def dispatch(r, carry):
        routing = tokb[r, pl.ds(TOK, META), :].astype(F32)
        places, shares = [], []
        for e in range(2):
            number = (ex * 2 + e).astype(F32)
            named = jnp.zeros((1, TOK), F32)
            weight = jnp.zeros((1, TOK), F32)
            for k in range(TOP):
                cols = slice(k * TOK, (k + 1) * TOK)
                hit = routing[0:1, cols] == number
                value = routing[1:2, cols] + routing[2:3, cols] + routing[3:4, cols]
                named = named + jnp.where(hit, 1.0, 0.0)
                weight = weight + jnp.where(hit, value, 0.0)
            many = jnp.broadcast_to(named, (16, TOK)).astype(BF16)
            slot = jnp.dot(many, tri[...], preferred_element_type=F32)[0:1, :]
            place = jnp.where(slot_number == slot, jnp.broadcast_to(named, (CAP, TOK)), 0.0)
            places.append(place)
            shares.append(place * weight)
        share = jnp.concatenate(shares, axis=0).T
        upper = share.astype(BF16)
        pt[0, r, :, :] = upper
        pt[1, r, :, :] = (share - upper.astype(F32)).astype(BF16)
        place = jnp.concatenate(places, axis=0).astype(BF16)
        rows = pl.ds(pl.multiple_of(r * CAP, CAP), CAP)
        for c in range(4):
            cols = slice(c * 512, (c + 1) * 512)
            picked = jnp.dot(place, tokb[r, 0:TOK, cols], preferred_element_type=F32).astype(BF16)
            xs[0, rows, cols] = picked[0:CAP]
            xs[1, rows, cols] = picked[CAP:]
        return carry

    def gate_up(p):
        e, n = PIECES[p]

        def tile(i, carry):
            rows = pl.ds(pl.multiple_of(i * 640, 640), 640)
            both = jnp.dot(xs[e, rows, :], wg[e, n].reshape(D, 2 * COL), preferred_element_type=F32)
            gate, up = both[:, :COL], both[:, COL:]
            hid[e, rows, n * COL : (n + 1) * COL] = (gate / (1.0 + jnp.exp(-gate)) * up).astype(BF16)
            return carry

        lax.fori_loop(0, 2, tile, 0)

    def own_piece(p):
        loads[(p, 0)].wait()
        loads[(p, 1)].wait()
        start(gu[p]["right"], gu[p]["left"])

    def forward(p):
        wait(gu[p]["right"], gu[p]["left"])
        start(gu[p]["fwd_r"], gu[p]["fwd_l"])

    def far_forward(p):
        wait(gu[p]["zright"], gu[p]["zleft"])
        start(gu[p]["zfwd_r"], gu[p]["zfwd_l"])

    def far_start(p):
        wait(gu[p]["z"])
        start(gu[p]["zright"], gu[p]["zleft"])

    own_piece(4)
    loads["tok"].wait()
    start(t_z, t_right, t_left, twins[OWN])
    own_piece(5)
    for p in Z_FIRST:
        own_piece(p)
    start(gu[0]["z"], gu[1]["z"], gu[4]["z"], gu[5]["z"], gu[2]["z"])

    forward(4)
    forward(5)
    start(gu[4]["zl"], gu[5]["zl"], gu[3]["z"], gu[4]["zr"], gu[5]["zr"])
    forward(0)
    wait(t_right)
    start(t_fwd_r)
    wait(t_left)
    start(t_fwd_l)
    wait(t_z)
    start(t_zright, t_zleft, twins[ZED], twins[LEFT], twins[RIGHT])
    forward(1)
    forward(2)
    far_start(0)
    forward(3)
    for s in (OWN, ZED, LEFT, RIGHT):
        wait(twins[s])
    lax.fori_loop(0, 8, dispatch, 0)
    far_start(1)
    wait(t_fwd_r, t_fwd_l)
    start(twins[ACROSS])
    for p in X_FIRST:
        wait(gu[p]["fwd_r"], gu[p]["fwd_l"])
        start(gu[p]["za"])
    far_start(2)
    far_forward(0)
    wait(t_zright)
    start(t_zfwd_r)
    wait(t_zleft)
    start(t_zfwd_l, twins[ZLEFT], twins[ZRIGHT])
    far_forward(1)
    far_start(3)
    for s in (ACROSS, ZLEFT, ZRIGHT):
        wait(twins[s])
    lax.fori_loop(8, 14, dispatch, 0)
    far_forward(2)
    wait(t_zfwd_r, t_zfwd_l)
    start(twins[ZACROSS])
    wait(twins[ZACROSS])
    lax.fori_loop(14, SRC, dispatch, 0)
    for m in token_moves:
        m.wait_send()
    for peer in (y_right, y_left, z_near, twin):
        pl.semaphore_signal(free_sem, inc=1, device_id=peer, device_id_type=MESH)
    loads["down0"].wait()
    loads["down1"].wait()
    start(dn[0]["z"], dn[1]["z"])
    for name in ("fwd_r", "fwd_l", "zfwd_r", "zfwd_l"):
        wait(gu[0][name])
    gate_up(0)
    far_forward(3)
    start(dn[0]["right"], dn[0]["left"], dn[1]["right"], dn[1]["left"])
    for p in (1, 2, 3):
        for name in ("fwd_r", "fwd_l", "zfwd_r", "zfwd_l"):
            wait(gu[p][name])
        gate_up(p)
    for p in X_FIRST:
        for name in ("z", "zl", "zr", "za"):
            wait(gu[p][name])
        gate_up(p)
    pl.semaphore_wait(free_sem, 4)

    def is_z_first(c):
        return (c % 2 == 1) & (c < 6)

    def rows_at(c, first=0, rows=TOK):
        return pl.ds(pl.multiple_of((c % 4) * TOK + first, TOK // 2), rows)

    def theirs_at(c):
        return pl.ds(pl.multiple_of((c % 2) * TOK, TOK), TOK)

    upper, lower = pl.ds(0, TOK // 2), pl.ds(TOK // 2, TOK // 2)
    every = pl.ds(0, TOK)

    def lane(c, width):
        return pl.ds(pl.multiple_of((c % 4) * 512, 512), width)

    class Return:
        def __init__(self, c, z_first=False):
            width = COL if z_first else 2 * COL
            hop_src = [
                (xs.at[0, rows_at(c, 0, TOK // 2), pl.ds(2 * width, width)], y_right),
                (xs.at[0, rows_at(c, TOK // 2, TOK // 2), pl.ds(2 * width, width)], y_left),
                (xs.at[0, rows_at(c), pl.ds(width, width)], y_right),
                (xs.at[0, rows_at(c), pl.ds(3 * width, width)], y_left),
            ]
            hop_dst = [
                tokb.at[8 + c // 4, upper, lane(c, width)],
                tokb.at[8 + c // 4, lower, lane(c, width)],
                tokb.at[10 + c // 4, every, lane(c, width)],
                tokb.at[12 + c // 4, every, lane(c, width)],
            ]
            if z_first:
                z = (xs.at[0, rows_at(c), pl.ds(4 * COL, 4 * COL)], zbuf.at[c // 2], z_near)
            else:
                lands = tokb.at[14, every, pl.ds(pl.multiple_of(c * COL, COL), COL)]
                z = (xs.at[0, rows_at(c), pl.ds(COL, COL)], lands, z_near)
            self.moves = [
                (xs.at[1, theirs_at(c)], tokb.at[c, every], twin),
                *((src, dst, device) for (src, device), dst in zip(hop_src, hop_dst)),
                z,
            ]
            self.c, self.width = c, width

        def copy(self, k):
            src, dst, device = self.moves[k]
            return pltpu.make_async_remote_copy(
                src_ref=src, dst_ref=dst, send_sem=ret_send.at[k, self.c], recv_sem=ret_recv.at[k, self.c],
                device_id=device, device_id_type=MESH,
            )

        def start(self, *which):
            for k in which:
                self.copy(k).start()

        def wait(self, *which):
            for k in which:
                self.copy(k).wait_recv()

        def drain(self, *which):
            for k in which:
                self.copy(k).wait_send()

        def landed(self, k):
            return self.moves[k][1][...]

    def add(rows, cols, *more):
        total = xs[0, rows, cols].astype(F32)
        for m in more:
            total = total + m.astype(F32)
        return total

    def finish(c, total):
        column = ((zh + c // 4) % 2) * 4 + (x + 4 - c % 4) % 4
        out[:, pl.ds(pl.multiple_of(column * COL, COL), COL)] = total.astype(BF16)

    def stage_compute(c):
        @pl.when(c >= 2)
        def _():
            Return(c - 2).drain(0)

        for e in range(2):
            y_e = jnp.dot(hid[e], wd[e, c], preferred_element_type=F32).astype(BF16)
            yb[:, e * CAP : (e + 1) * CAP, :] = y_e.reshape(SRC, CAP, COL)
        kind = is_z_first(c).astype(jnp.int32)

        combine_into(c, kind, 1)
        Return(c).start(0)
        combine_into(c, kind, 0)

    def combine_into(c, kind, parity):
        for (yy, zz), s in RETURN.items():
            place = kind * (4 * zz + yy) + (1 - kind) * (2 * yy + zz)
            cols = pl.ds(pl.multiple_of(place * COL, COL), COL)
            r = s + parity
            total = jnp.dot(pt[0, r], yb[r], preferred_element_type=F32)
            total = total + jnp.dot(pt[1, r], yb[r], preferred_element_type=F32)
            if parity:
                xs[1, theirs_at(c), cols] = total.astype(BF16)
            else:
                xs[0, rows_at(c), cols] = total.astype(BF16)

    def stage_twin(c):
        Return(c).wait(0)

        def rows_of(i, carry):
            rows = pl.ds(pl.multiple_of((c % 4) * TOK + i * 32, 32), 32)
            got = tokb[c, pl.ds(pl.multiple_of(i * 32, 32), 32), :]
            xs[0, rows, :] = add(rows, slice(None), got).astype(BF16)
            return carry

        lax.fori_loop(0, TOK // 32, rows_of, 0)

        @pl.when(is_z_first(c))
        def _():
            Return(c, True).start(5)

        @pl.when(jnp.logical_not(is_z_first(c)))
        def _():
            Return(c).start(1, 2)

    def second_hop(move):
        c, width = move.c, move.width
        move.wait(1)
        rows, cols = rows_at(c, 0, TOK // 2), slice(width, 2 * width)
        xs[0, rows, cols] = add(rows, cols, move.landed(1)).astype(BF16)
        move.start(3)
        move.wait(2)
        rows, cols = rows_at(c, TOK // 2, TOK // 2), slice(3 * width, 4 * width)
        xs[0, rows, cols] = add(rows, cols, move.landed(2)).astype(BF16)
        move.start(4)

    def stage_second(c):
        @pl.when(is_z_first(c))
        def _():
            move = Return(c, True)
            move.wait(5)

            def rows_of(i, carry):
                rows = pl.ds(pl.multiple_of((c % 4) * TOK + i * 32, 32), 32)
                got = zbuf[c // 2, pl.ds(pl.multiple_of(i * 32, 32), 32), :]
                xs[0, rows, 0 : 4 * COL] = add(rows, slice(0, 4 * COL), got).astype(BF16)
                return carry

            lax.fori_loop(0, TOK // 32, rows_of, 0)
            move.start(1, 2)

        @pl.when(jnp.logical_not(is_z_first(c)))
        def _():
            second_hop(Return(c))

    def stage_third(c):
        @pl.when(is_z_first(c))
        def _():
            second_hop(Return(c, True))

        @pl.when(jnp.logical_not(is_z_first(c)))
        def _():
            move = Return(c)
            move.wait(3, 4)
            cols = slice(0, 2 * COL)
            total = add(rows_at(c), cols, move.landed(3), move.landed(4))
            xs[0, rows_at(c), cols] = total.astype(BF16)
            move.start(5)

    def stage_last(c):
        @pl.when(is_z_first(c))
        def _():
            move = Return(c, True)
            move.wait(3, 4)
            finish(c, add(rows_at(c), slice(0, COL), move.landed(3), move.landed(4)))
            move.drain(1, 2, 3, 4, 5)

        @pl.when(jnp.logical_not(is_z_first(c)))
        def _():
            move = Return(c)
            move.wait(5)
            finish(c, add(rows_at(c), slice(0, COL), move.landed(5)))
            move.drain(1, 2, 3, 4, 5)

    def step(i, carry):
        @pl.when(i == 1)
        def _():
            for e in range(2):
                wait(dn[e]["right"], dn[e]["left"])
                start(dn[e]["fwd_r"], dn[e]["fwd_l"])

        @pl.when(i == 2)
        def _():
            for e in range(2):
                wait(dn[e]["z"])
                start(dn[e]["zright"], dn[e]["zleft"])
            for e in range(2):
                wait(dn[e]["fwd_r"], dn[e]["fwd_l"])

        @pl.when(i == 5)
        def _():
            for e in range(2):
                wait(dn[e]["zright"], dn[e]["zleft"])
                start(dn[e]["zfwd_r"], dn[e]["zfwd_l"])

        @pl.when(i == 6)
        def _():
            for e in range(2):
                wait(dn[e]["zfwd_r"], dn[e]["zfwd_l"])

        @pl.when(i < STEPS)
        def _():
            stage_compute(i)

        @pl.when(i < STEPS)
        def _():
            stage_twin(i)

        @pl.when((i >= 1) & (i < STEPS + 1))
        def _():
            stage_second(i - 1)

        @pl.when((i >= 2) & (i < STEPS + 2))
        def _():
            stage_third(i - 2)

        @pl.when(i >= 3)
        def _():
            stage_last(i - 3)

        return carry

    lax.fori_loop(0, STEPS + 3, step, 0)
    Return(STEPS - 2).drain(0)
    Return(STEPS - 1).drain(0)
    for group in (*gu, *dn):
        for m in group.values():
            m.wait_send()


def shards(tokens, expert_ids, route_probs, w_gate_up, w_down):
    any_spec = pl.BlockSpec(memory_space=pl.ANY)
    vmem_spec = pl.BlockSpec(memory_space=pltpu.VMEM)
    return pl.pallas_call(
        kernel,
        out_shape=jax.ShapeDtypeStruct((TOK, D), BF16),
        in_specs=[any_spec, vmem_spec, vmem_spec, any_spec, any_spec],
        out_specs=vmem_spec,
        scratch_shapes=[
            pltpu.VMEM((SRC, ROWS, D), BF16),
            pltpu.VMEM((2, 3, STEPS, COL, 2 * COL), BF16),
            pltpu.VMEM((2, STEPS, FF, COL), BF16),
            pltpu.VMEM((2, SRC * CAP, D), BF16),
            pltpu.VMEM((2, SRC * CAP, FF), BF16),
            pltpu.VMEM((2, SRC, TOK, 2 * CAP), BF16),
            pltpu.VMEM((SRC, 2 * CAP, COL), BF16),
            pltpu.VMEM((TOK, TOK), BF16),
            pltpu.VMEM((3, TOK, 4 * COL), BF16),
            pltpu.SemaphoreType.DMA((15,)),
            pltpu.SemaphoreType.DMA((MOVES,)),
            pltpu.SemaphoreType.DMA((MOVES,)),
            pltpu.SemaphoreType.DMA((6, STEPS)),
            pltpu.SemaphoreType.DMA((6, STEPS)),
            pltpu.SemaphoreType.REGULAR,
        ],
        compiler_params=pltpu.CompilerParams(
            collective_id=0, has_side_effects=True, vmem_limit_bytes=67_000_000
        ),
    )(tokens, expert_ids.T, route_probs.T, w_gate_up, w_down)


def solution(mesh):
    spec = P(("dp", "expert"), None)
    in_specs = (spec, spec, spec, P("expert", "dp", None), P("expert", None, "dp"))
    return jax.shard_map(shards, mesh=mesh, in_specs=in_specs, out_specs=spec, check_vma=False)
```

time: 576 us -> 201 us (0.35)
  the two profiles are of different devices: /device:TPU:49 before, /device:TPU:0 now
where the time goes in v1:
time: 201 us; the launch traced here: 200 us
  Pallas kernels  198 us (99%)
  local copies, waits for them, and re-layouts  2.3 us (1%)
    pallas_call x1, Pallas kernels, shards(): pl.pallas_call(kernel, out_shape=jax.ShapeDtypeStruct((TOK, D), BF16), in...  198 us

profile of v1, /device:TPU:0, one launch (start us, length us, event | category | flops | bytes accessed | tf_op | source)
XLA Modules:
  0.0 200.3 jit_solution(6305671055148769611)
XLA Ops:
  0.0 198.0 %shard_map.55 = bf16[256,2048]{1,0:T(8,128)(2,1)} custom-call(bf16[256,2048]{1,0:T(8,128)(2,1)} %tok.1, s32[8,256]{1,0:T(8,128)} %bitcast.2, f32[8,256]{1,0:T(8,128)} %bitcast.3, bf16[2,256,1536]{2,1,0:T(8,128)(2,1)} %wgu.1, bf16[2,768,256]{2,1,0:T(8,128)(2,1)} %wdn.1), custom_call_target="tpu_custom_call" | custom-call | tf_op jit(solution)/shard_map/pallas_call | solution.py:549
  198.0 2.3 %copy.7 = bf16[256,2048]{1,0:T(8,128)(2,1)} copy(bf16[256,2048]{1,0:T(8,128)(2,1)} %shard_map.55) | data formatting | bytes 2097152

commit v2 on v1

--- a/solution.py
+++ b/solution.py
@@ -20,7 +20,7 @@
 SRC = 16
 COL = 256
 STEPS = 8
-MOVES = 17 + 4 * 9 + 2 * 8 + 2 * 9
+MOVES = 17 + 4 * 9 + 8 + 9 + 2 * 9
 
 OWN, ZED, LEFT, RIGHT, ACROSS, ZLEFT, ZRIGHT, ZACROSS = range(0, 16, 2)
 RETURN = {
@@ -30,6 +30,17 @@
 PIECES = [(e, n) for e in range(2) for n in range(3)]
 Z_FIRST = (0, 1, 2, 3)
 X_FIRST = (4, 5)
+Z_ACROSS = 4
+
+DOWN = (0, 1, 3, 4, 2, 5, 7, 6)
+RETURN_Z_FIRST = (1, 4, 6)
+PLAN = (
+    ("n", 0), ("C", 0), ("T", 0), ("n", 1), ("f", 0), ("C", 1), ("S", 0), ("T", 1), ("C", 2), ("f", 1),
+    ("C", 3), ("T", 2), ("T", 3), ("H", 0), ("a", 0), ("a", 1), ("C", 4), ("S", 2), ("T", 4), ("S", 1),
+    ("F", 0), ("S", 3), ("L", 0), ("H", 2), ("H", 1), ("F", 1), ("C", 5), ("C", 6), ("T", 5), ("S", 4), ("T", 6),
+    ("H", 3), ("S", 5), ("L", 2), ("L", 1), ("A", 0), ("A", 1), ("H", 4), ("C", 7), ("T", 7), ("H", 5), ("S", 6), ("S", 7),
+    ("H", 6), ("L", 4), ("L", 3), ("L", 5), ("H", 7), ("L", 6), ("L", 7),
+)
 
 
 def kernel(
@@ -95,7 +106,7 @@
     twins = {s: block(s, s + 1, twin) for s in range(0, SRC, 2)}
     token_moves = [t_z, t_right, t_left, t_fwd_r, t_fwd_l, t_zright, t_zleft, t_zfwd_r, t_zfwd_l, *twins.values()]
 
-    def gate_up_moves(e, n, x_first):
+    def gate_up_moves(e, n, x_first, z_across):
         def move(device, sends, takes, rows=None):
             src, lands = wg.at[e, n, sends[0] * 4 + sends[1]], wg.at[e, n, takes[0] * 4 + takes[1]]
             if rows is not None:
@@ -112,11 +123,15 @@
         if x_first:
             moves.update(
                 zl=move(z_far, (zh, xl), (far, xl)), zr=move(z_far, (zh, xr), (far, xr)),
-                za=move(z_far, (zh, xa), (far, xa)),
             )
         else:
             moves.update(
                 zright=move(x_right, (far, x), (far, xl)), zleft=move(x_left, (far, x), (far, xr)),
+            )
+        if z_across:
+            moves.update(za=move(z_far, (zh, xa), (far, xa)))
+        else:
+            moves.update(
                 zfwd_r=move(x_right, (far, xl), (far, xa), top), zfwd_l=move(x_left, (far, xr), (far, xa), low),
             )
         return moves
@@ -136,7 +151,7 @@
             zfwd_r=move(x_right, 5, 6, top), zfwd_l=move(x_left, 7, 6, low),
         )
 
-    gu = [gate_up_moves(e, n, p in X_FIRST) for p, (e, n) in enumerate(PIECES)]
+    gu = [gate_up_moves(e, n, p in X_FIRST, p == Z_ACROSS) for p, (e, n) in enumerate(PIECES)]
     dn = [down_moves(0), down_moves(1)]
 
     mine = zh * 4 + x
@@ -211,7 +226,7 @@
             xs[1, rows, cols] = picked[CAP:]
         return carry
 
-    def gate_up(p):
+    def gate_up(p, *halves):
         e, n = PIECES[p]
 
         def tile(i, carry):
@@ -221,7 +236,7 @@
             hid[e, rows, n * COL : (n + 1) * COL] = (gate / (1.0 + jnp.exp(-gate)) * up).astype(BF16)
             return carry
 
-        lax.fori_loop(0, 2, tile, 0)
+        lax.fori_loop(halves[0], halves[-1] + 1, tile, 0)
 
     def own_piece(p):
         loads[(p, 0)].wait()
@@ -239,6 +254,12 @@
     def far_start(p):
         wait(gu[p]["z"])
         start(gu[p]["zright"], gu[p]["zleft"])
+
+    def whole_piece(p):
+        names = [k for k in gu[p] if k.startswith(("fwd", "zfwd", "za"))]
+        if p in X_FIRST:
+            names = [k for k in names if not k.startswith("fwd")] + ["z"] + (["zl", "zr"] if p == Z_ACROSS else [])
+        wait(*(gu[p][k] for k in names))
 
     own_piece(4)
     loads["tok"].wait()
@@ -270,7 +291,8 @@
     start(twins[ACROSS])
     for p in X_FIRST:
         wait(gu[p]["fwd_r"], gu[p]["fwd_l"])
-        start(gu[p]["za"])
+        if p == Z_ACROSS:
+            start(gu[p]["za"])
     far_start(2)
     far_forward(0)
     wait(t_zright)
@@ -278,6 +300,8 @@
     wait(t_zleft)
     start(t_zfwd_l, twins[ZLEFT], twins[ZRIGHT])
     far_forward(1)
+    whole_piece(0)
+    gate_up(0, 0)
     far_start(3)
     for s in (ACROSS, ZLEFT, ZRIGHT):
         wait(twins[s])
@@ -285,8 +309,11 @@
     far_forward(2)
     wait(t_zfwd_r, t_zfwd_l)
     start(twins[ZACROSS])
+    whole_piece(1)
+    gate_up(1, 0)
     wait(twins[ZACROSS])
     lax.fori_loop(14, SRC, dispatch, 0)
+    gate_up(0, 1)
     for m in token_moves:
         m.wait_send()
     for peer in (y_right, y_left, z_near, twin):
@@ -294,250 +321,183 @@
     loads["down0"].wait()
     loads["down1"].wait()
     start(dn[0]["z"], dn[1]["z"])
-    for name in ("fwd_r", "fwd_l", "zfwd_r", "zfwd_l"):
-        wait(gu[0][name])
-    gate_up(0)
+    gate_up(1, 1)
     far_forward(3)
+    whole_piece(2)
+    gate_up(2, 0, 1)
+    wait(gu[5]["zl"], gu[5]["zr"])
+    start(gu[5]["zfwd_r"], gu[5]["zfwd_l"])
     start(dn[0]["right"], dn[0]["left"], dn[1]["right"], dn[1]["left"])
-    for p in (1, 2, 3):
-        for name in ("fwd_r", "fwd_l", "zfwd_r", "zfwd_l"):
-            wait(gu[p][name])
-        gate_up(p)
-    for p in X_FIRST:
-        for name in ("z", "zl", "zr", "za"):
-            wait(gu[p][name])
-        gate_up(p)
+    for p in (3, 4, 5):
+        whole_piece(p)
+        gate_up(p, 0, 1)
     pl.semaphore_wait(free_sem, 4)
 
-    def is_z_first(c):
-        return (c % 2 == 1) & (c < 6)
-
-    def rows_at(c, first=0, rows=TOK):
-        return pl.ds(pl.multiple_of((c % 4) * TOK + first, TOK // 2), rows)
-
-    def theirs_at(c):
-        return pl.ds(pl.multiple_of((c % 2) * TOK, TOK), TOK)
+    def own_rows(c, first=0, rows=TOK):
+        e, at = (0, c) if c < 5 else (1, c - 3)
+        return e, pl.ds(at * TOK + first, rows)
 
     upper, lower = pl.ds(0, TOK // 2), pl.ds(TOK // 2, TOK // 2)
     every = pl.ds(0, TOK)
 
-    def lane(c, width):
-        return pl.ds(pl.multiple_of((c % 4) * 512, 512), width)
-
     class Return:
-        def __init__(self, c, z_first=False):
-            width = COL if z_first else 2 * COL
-            hop_src = [
-                (xs.at[0, rows_at(c, 0, TOK // 2), pl.ds(2 * width, width)], y_right),
-                (xs.at[0, rows_at(c, TOK // 2, TOK // 2), pl.ds(2 * width, width)], y_left),
-                (xs.at[0, rows_at(c), pl.ds(width, width)], y_right),
-                (xs.at[0, rows_at(c), pl.ds(3 * width, width)], y_left),
-            ]
-            hop_dst = [
-                tokb.at[8 + c // 4, upper, lane(c, width)],
-                tokb.at[8 + c // 4, lower, lane(c, width)],
-                tokb.at[10 + c // 4, every, lane(c, width)],
-                tokb.at[12 + c // 4, every, lane(c, width)],
-            ]
-            if z_first:
-                z = (xs.at[0, rows_at(c), pl.ds(4 * COL, 4 * COL)], zbuf.at[c // 2], z_near)
+        def __init__(self, c):
+            self.c, self.z_first = c, c in RETURN_Z_FIRST
+            self.width = width = COL if self.z_first else 2 * COL
+            lane = pl.ds(c % 4 * 512, width)
+
+            def mine(col, cols, first=0, rows=TOK):
+                e, at = own_rows(c, first, rows)
+                return xs.at[e, at, pl.ds(col, cols)]
+
+            if self.z_first:
+                z = (mine(4 * COL, 4 * COL), zbuf.at[RETURN_Z_FIRST.index(c)], z_near)
             else:
-                lands = tokb.at[14, every, pl.ds(pl.multiple_of(c * COL, COL), COL)]
-                z = (xs.at[0, rows_at(c), pl.ds(COL, COL)], lands, z_near)
-            self.moves = [
-                (xs.at[1, theirs_at(c)], tokb.at[c, every], twin),
-                *((src, dst, device) for (src, device), dst in zip(hop_src, hop_dst)),
-                z,
-            ]
-            self.c, self.width = c, width
-
-        def copy(self, k):
-            src, dst, device = self.moves[k]
+                z = (mine(COL, COL), tokb.at[14, every, pl.ds(c * COL, COL)], z_near)
+            half = TOK // 2
+            self.moves = dict(
+                twin=(xs.at[1, pl.ds(c % 2 * TOK, TOK)], tokb.at[c, every], twin),
+                right1=(mine(2 * width, width, 0, half), tokb.at[8 + c // 4, upper, lane], y_right),
+                left1=(mine(2 * width, width, half, half), tokb.at[8 + c // 4, lower, lane], y_left),
+                right2=(mine(width, width), tokb.at[10 + c // 4, every, lane], y_right),
+                left2=(mine(3 * width, width), tokb.at[12 + c // 4, every, lane], y_left),
+                z=z,
+            )
+            self.names = list(self.moves)
+
+        def copy(self, name):
+            (src, dst, device), k = self.moves[name], self.names.index(name)
             return pltpu.make_async_remote_copy(
                 src_ref=src, dst_ref=dst, send_sem=ret_send.at[k, self.c], recv_sem=ret_recv.at[k, self.c],
                 device_id=device, device_id_type=MESH,
             )
 
-        def start(self, *which):
-            for k in which:
-                self.copy(k).start()
-
-        def wait(self, *which):
-            for k in which:
-                self.copy(k).wait_recv()
-
-        def drain(self, *which):
-            for k in which:
-                self.copy(k).wait_send()
-
-        def landed(self, k):
-            return self.moves[k][1][...]
-
-    def add(rows, cols, *more):
-        total = xs[0, rows, cols].astype(F32)
-        for m in more:
-            total = total + m.astype(F32)
-        return total
-
-    def finish(c, total):
-        column = ((zh + c // 4) % 2) * 4 + (x + 4 - c % 4) % 4
-        out[:, pl.ds(pl.multiple_of(column * COL, COL), COL)] = total.astype(BF16)
-
-    def stage_compute(c):
-        @pl.when(c >= 2)
-        def _():
-            Return(c - 2).drain(0)
-
-        for e in range(2):
-            y_e = jnp.dot(hid[e], wd[e, c], preferred_element_type=F32).astype(BF16)
-            yb[:, e * CAP : (e + 1) * CAP, :] = y_e.reshape(SRC, CAP, COL)
-        kind = is_z_first(c).astype(jnp.int32)
-
-        combine_into(c, kind, 1)
-        Return(c).start(0)
-        combine_into(c, kind, 0)
-
-    def combine_into(c, kind, parity):
-        for (yy, zz), s in RETURN.items():
-            place = kind * (4 * zz + yy) + (1 - kind) * (2 * yy + zz)
-            cols = pl.ds(pl.multiple_of(place * COL, COL), COL)
-            r = s + parity
-            total = jnp.dot(pt[0, r], yb[r], preferred_element_type=F32)
-            total = total + jnp.dot(pt[1, r], yb[r], preferred_element_type=F32)
-            if parity:
-                xs[1, theirs_at(c), cols] = total.astype(BF16)
+        def start(self, *names):
+            for name in names:
+                self.copy(name).start()
+
+        def wait_recv(self, *names):
+            for name in names:
+                self.copy(name).wait_recv()
+
+        def wait_send(self, *names):
+            for name in names:
+                self.copy(name).wait_send()
+
+        def landed(self, name):
+            return self.moves[name][1][...].astype(F32)
+
+        def place(self, yy, zz):
+            return 4 * zz + yy if self.z_first else 2 * yy + zz
+
+        def combine(self, parity):
+            for (yy, zz), s in RETURN.items():
+                cols = slice(self.place(yy, zz) * COL, (self.place(yy, zz) + 1) * COL)
+                r = s + parity
+                total = jnp.dot(pt[0, r], yb[r], preferred_element_type=F32)
+                total = total + jnp.dot(pt[1, r], yb[r], preferred_element_type=F32)
+                if parity:
+                    xs[1, pl.ds(self.c % 2 * TOK, TOK), cols] = total.astype(BF16)
+                else:
+                    e, rows = own_rows(self.c)
+                    xs[e, rows, cols] = total.astype(BF16)
+
+        def compute(self):
+            if self.c >= 2:
+                returns[self.c - 2].wait_send("twin")
+            for e in range(2):
+                y_e = jnp.dot(hid[e], wd[e, DOWN[self.c]], preferred_element_type=F32).astype(BF16)
+                yb[:, e * CAP : (e + 1) * CAP, :] = y_e.reshape(SRC, CAP, COL)
+            self.combine(1)
+            self.start("twin")
+            self.combine(0)
+
+        def add(self, theirs, cols):
+            e, rows = own_rows(self.c)
+
+            def some(i, carry):
+                at = pl.ds(pl.multiple_of(rows.start + i * 32, 32), 32)
+                got = theirs[pl.ds(pl.multiple_of(i * 32, 32), 32), :].astype(F32)
+                xs[e, at, 0:cols] = (xs[e, at, 0:cols].astype(F32) + got).astype(BF16)
+                return carry
+
+            lax.fori_loop(0, TOK // 32, some, 0)
+
+        def join_twin(self):
+            self.wait_recv("twin")
+            self.add(tokb.at[self.c], D)
+            self.start(*(("z",) if self.z_first else ("right1", "left1")))
+
+        def second(self):
+            width, half = self.width, TOK // 2
+            for there, col, first in (("right", width, 0), ("left", 3 * width, half)):
+                self.wait_recv(there + "1")
+                e, rows = own_rows(self.c, first, half)
+                total = xs[e, rows, col : col + width].astype(F32) + self.landed(there + "1")
+                xs[e, rows, col : col + width] = total.astype(BF16)
+                self.start(there + "2")
+
+        def home(self):
+            self.wait_recv("right2", "left2")
+            e, rows = own_rows(self.c)
+            return xs[e, rows, 0 : self.width].astype(F32) + self.landed("right2") + self.landed("left2")
+
+        def hop(self):
+            if self.z_first:
+                self.wait_recv("z")
+                self.add(zbuf.at[RETURN_Z_FIRST.index(self.c)], 4 * COL)
+                self.start("right1", "left1")
             else:
-                xs[0, rows_at(c), cols] = total.astype(BF16)
-
-    def stage_twin(c):
-        Return(c).wait(0)
-
-        def rows_of(i, carry):
-            rows = pl.ds(pl.multiple_of((c % 4) * TOK + i * 32, 32), 32)
-            got = tokb[c, pl.ds(pl.multiple_of(i * 32, 32), 32), :]
-            xs[0, rows, :] = add(rows, slice(None), got).astype(BF16)
-            return carry
-
-        lax.fori_loop(0, TOK // 32, rows_of, 0)
-
-        @pl.when(is_z_first(c))
-        def _():
-            Return(c, True).start(5)
-
-        @pl.when(jnp.logical_not(is_z_first(c)))
-        def _():
-            Return(c).start(1, 2)
-
-    def second_hop(move):
-        c, width = move.c, move.width
-        move.wait(1)
-        rows, cols = rows_at(c, 0, TOK // 2), slice(width, 2 * width)
-        xs[0, rows, cols] = add(rows, cols, move.landed(1)).astype(BF16)
-        move.start(3)
-        move.wait(2)
-        rows, cols = rows_at(c, TOK // 2, TOK // 2), slice(3 * width, 4 * width)
-        xs[0, rows, cols] = add(rows, cols, move.landed(2)).astype(BF16)
-        move.start(4)
-
-    def stage_second(c):
-        @pl.when(is_z_first(c))
-        def _():
-            move = Return(c, True)
-            move.wait(5)
-
-            def rows_of(i, carry):
-                rows = pl.ds(pl.multiple_of((c % 4) * TOK + i * 32, 32), 32)
-                got = zbuf[c // 2, pl.ds(pl.multiple_of(i * 32, 32), 32), :]
-                xs[0, rows, 0 : 4 * COL] = add(rows, slice(0, 4 * COL), got).astype(BF16)
-                return carry
-
-            lax.fori_loop(0, TOK // 32, rows_of, 0)
-            move.start(1, 2)
-
-        @pl.when(jnp.logical_not(is_z_first(c)))
-        def _():
-            second_hop(Return(c))
-
-    def stage_third(c):
-        @pl.when(is_z_first(c))
-        def _():
-            second_hop(Return(c, True))
-
-        @pl.when(jnp.logical_not(is_z_first(c)))
-        def _():
-            move = Return(c)
-            move.wait(3, 4)
-            cols = slice(0, 2 * COL)
-            total = add(rows_at(c), cols, move.landed(3), move.landed(4))
-            xs[0, rows_at(c), cols] = total.astype(BF16)
-            move.start(5)
-
-    def stage_last(c):
-        @pl.when(is_z_first(c))
-        def _():
-            move = Return(c, True)
-            move.wait(3, 4)
-            finish(c, add(rows_at(c), slice(0, COL), move.landed(3), move.landed(4)))
-            move.drain(1, 2, 3, 4, 5)
-
-        @pl.when(jnp.logical_not(is_z_first(c)))
-        def _():
-            move = Return(c)
-            move.wait(5)
-            finish(c, add(rows_at(c), slice(0, COL), move.landed(5)))
-            move.drain(1, 2, 3, 4, 5)
-
-    def step(i, carry):
-        @pl.when(i == 1)
-        def _():
-            for e in range(2):
-                wait(dn[e]["right"], dn[e]["left"])
-                start(dn[e]["fwd_r"], dn[e]["fwd_l"])
-
-        @pl.when(i == 2)
-        def _():
-            for e in range(2):
-                wait(dn[e]["z"])
-                start(dn[e]["zright"], dn[e]["zleft"])
-            for e in range(2):
-                wait(dn[e]["fwd_r"], dn[e]["fwd_l"])
-
-        @pl.when(i == 5)
-        def _():
-            for e in range(2):
-                wait(dn[e]["zright"], dn[e]["zleft"])
-                start(dn[e]["zfwd_r"], dn[e]["zfwd_l"])
-
-        @pl.when(i == 6)
-        def _():
-            for e in range(2):
-                wait(dn[e]["zfwd_r"], dn[e]["zfwd_l"])
-
-        @pl.when(i < STEPS)
-        def _():
-            stage_compute(i)
-
-        @pl.when(i < STEPS)
-        def _():
-            stage_twin(i)
-
-        @pl.when((i >= 1) & (i < STEPS + 1))
-        def _():
-            stage_second(i - 1)
-
-        @pl.when((i >= 2) & (i < STEPS + 2))
-        def _():
-            stage_third(i - 2)
-
-        @pl.when(i >= 3)
-        def _():
-            stage_last(i - 3)
-
-        return carry
-
-    lax.fori_loop(0, STEPS + 3, step, 0)
-    Return(STEPS - 2).drain(0)
-    Return(STEPS - 1).drain(0)
+                self.second()
+
+        def third(self):
+            if self.z_first:
+                self.second()
+            else:
+                total = self.home()
+                e, rows = own_rows(self.c)
+                xs[e, rows, 0 : self.width] = total.astype(BF16)
+                self.start("z")
+
+        def last(self):
+            if self.z_first:
+                total = self.home()
+            else:
+                self.wait_recv("z")
+                e, rows = own_rows(self.c)
+                total = xs[e, rows, 0:COL].astype(F32) + self.landed("z")
+            slot = DOWN[self.c]
+            column = ((zh + slot // 4) % 2) * 4 + (x + 4 - slot % 4) % 4
+            out[:, pl.ds(pl.multiple_of(column * COL, COL), COL)] = total.astype(BF16)
+
+    def down_near(e):
+        wait(dn[e]["right"], dn[e]["left"])
+        start(dn[e]["fwd_r"], dn[e]["fwd_l"])
+
+    def down_far(e):
+        wait(dn[e]["z"])
+        start(dn[e]["zright"], dn[e]["zleft"])
+
+    def down_across(e):
+        wait(dn[e]["fwd_r"], dn[e]["fwd_l"])
+
+    def down_far_forward(e):
+        wait(dn[e]["zright"], dn[e]["zleft"])
+        start(dn[e]["zfwd_r"], dn[e]["zfwd_l"])
+
+    def down_far_across(e):
+        wait(dn[e]["zfwd_r"], dn[e]["zfwd_l"])
+
+    returns = [Return(c) for c in range(STEPS)]
+    do = {
+        "C": lambda c: returns[c].compute(), "T": lambda c: returns[c].join_twin(),
+        "S": lambda c: returns[c].hop(), "H": lambda c: returns[c].third(), "L": lambda c: returns[c].last(),
+        "n": down_near, "f": down_far, "a": down_across, "F": down_far_forward, "A": down_far_across,
+    }
+    for what, n in PLAN:
+        do[what](n)
+    for c in range(STEPS):
+        returns[c].wait_send(*returns[c].names[0 if c >= STEPS - 2 else 1 :])
     for group in (*gu, *dn):
         for m in group.values():
             m.wait_send()

time: 201 us -> 184 us (0.915)
  Pallas kernels: 198 us -> 182 us
    pallas_call x1, Pallas kernels: 198 us -> 182 us  [shards(): pl.pallas_call(kernel, out_shape=jax.ShapeDtypeStruct((TOK, D), BF16), in...]
where the time goes in v2:
time: 184 us
  Pallas kernels  182 us (99%)
  local copies, waits for them, and re-layouts  2.3 us (1%)
    pallas_call x1, Pallas kernels, shards(): pl.pallas_call(kernel, out_shape=jax.ShapeDtypeStruct((TOK, D), BF16), in...  182 us

profile of v2, /device:TPU:0, one launch (start us, length us, event | category | flops | bytes accessed | tf_op | source)
XLA Modules:
  0.0 184.2 jit_solution(16804847085860234759)
XLA Ops:
  0.0 181.9 %shard_map.55 = bf16[256,2048]{1,0:T(8,128)(2,1)} custom-call(bf16[256,2048]{1,0:T(8,128)(2,1)} %tok.1, s32[8,256]{1,0:T(8,128)} %bitcast.2, f32[8,256]{1,0:T(8,128)} %bitcast.3, bf16[2,256,1536]{2,1,0:T(8,128)(2,1)} %wgu.1, bf16[2,768,256]{2,1,0:T(8,128)(2,1)} %wdn.1), custom_call_target="tpu_custom_call" | custom-call | tf_op jit(solution)/shard_map/pallas_call | solution.py:509
  181.9 2.3 %copy.7 = bf16[256,2048]{1,0:T(8,128)(2,1)} copy(bf16[256,2048]{1,0:T(8,128)(2,1)} %shard_map.55) | data formatting | bytes 2097152

commit v3 on v2

v3 whole, which is shorter than its diff:
```python
import functools

import jax
import jax.numpy as jnp
from jax import lax
from jax.experimental import pallas as pl
from jax.experimental.pallas import tpu as pltpu
from jax.sharding import PartitionSpec as P

MESH = pl.DeviceIdType.MESH
F32 = jnp.float32
BF16 = jnp.bfloat16

TOK = 256
META = 16
ROWS = TOK + META
HALF = 144
D = 2048
FF = 768
TOP = 8
CAP = 80
SRC = 16
COL = 256
SHARDS = 8
STEPS = 16
STEP = COL // 2
LANDINGS = 8 + 4 * 4 + 3 + 4 + 2 * 5 + 16 * 4
SENDS = 1 + 6 + 2 + 1 + 4

OWN, ZED, LEFT, RIGHT, ACROSS, ZLEFT, ZRIGHT, ZACROSS = range(0, 16, 2)
RETURN = {
    (0, 0): OWN, (0, 1): ZED, (1, 0): RIGHT, (1, 1): ZRIGHT,
    (2, 0): ACROSS, (2, 1): ZACROSS, (3, 0): LEFT, (3, 1): ZLEFT,
}
PIECES = [(e, n) for e in range(2) for n in range(3)]
Z_FIRST = (0, 1, 2, 3)
X_FIRST = (4, 5)
Z_ACROSS = 4

UNITS = (
    ((0, 0), (0, 1)), ((1, 0), (3, 0)), ((1, 1), (3, 1)), ((4, 0), (4, 1)), ((2, 0), (2, 1)), ((5, 0), (7, 0)), ((5, 1), (7, 1)), ((6, 0),), ((6, 1),),
)
RETURN_Z_FIRST = (4, 6, 10, 12, 14)
Z_LAST = ()
PLAN = (
    ("C", 0), ("T", 0), ("T", 1), ("S", 0), ("n", 0), ("S", 1), ("C", 1), ("T", 2), ("T", 3), ("H", 1),
    ("n", 1), ("f", 0), ("f", 1), ("S", 2), ("H", 0), ("C", 2), ("C", 3), ("T", 4), ("T", 5), ("S", 3),
    ("T", 6), ("C", 4), ("S", 5), ("T", 9), ("S", 4), ("H", 3), ("T", 8), ("T", 7), ("S", 9), ("C", 5),
    ("S", 8), ("S", 6), ("H", 5), ("F", 0), ("L", 3), ("H", 4), ("T", 10), ("T", 11), ("H", 9), ("S", 7),
    ("F", 1), ("C", 6), ("T", 12), ("S", 11), ("C", 7), ("T", 13), ("S", 10), ("H", 6), ("T", 14), ("C", 8),
    ("T", 15), ("S", 13), ("S", 12), ("H", 11), ("L", 4), ("L", 9), ("S", 15), ("L", 6), ("H", 8), ("S", 14),
    ("H", 13), ("H", 12), ("H", 7), ("H", 10), ("L", 1), ("H", 2), ("L", 11), ("L", 5), ("L", 0), ("H", 15),
    ("H", 14), ("L", 10), ("L", 2), ("L", 12), ("L", 7), ("L", 13), ("L", 8), ("L", 15), ("L", 14),
)


def kernel(
    tok, ids, probs, wgu, wdn, out,
    tokb, wg, wd, xs, hid, pt, yb, tri, zbuf, ob, part,
    local_sem, send_sem, recv_sem, out_sem, free_sem,
):
    dp, ex = lax.axis_index("dp"), lax.axis_index("expert")
    zh, x = dp // 4, dp % 4
    y, zl, core = ex // 4, (ex // 2) % 2, ex % 2
    xl, xr, xa = (x + 3) % 4, (x + 1) % 4, (x + 2) % 4

    def at_dp(zhi, xx):
        return (zhi * 4 + xx, ex)

    def at_ex(yy, zz, cc):
        return (dp, (yy * 2 + zz) * 2 + cc)

    x_right, x_left, z_far = at_dp(zh, xr), at_dp(zh, xl), at_dp(1 - zh, x)
    y_right, y_left = at_ex((y + 1) % 4, zl, core), at_ex((y + 3) % 4, zl, core)
    z_near, twin = at_ex(y, 1 - zl, core), at_ex(y, zl, 1 - core)

    counts = dict(send=0, recv=0)

    def semaphore(kind):
        counts[kind] += 1
        return (send_sem if kind == "send" else recv_sem).at[counts[kind] - 1]

    def described(src, dst, send, recv, device):
        return pltpu.make_async_remote_copy(
            src_ref=src, dst_ref=dst, send_sem=send, recv_sem=recv, device_id=device, device_id_type=MESH
        )

    class Landing:
        def __init__(self, ref):
            self.ref, self.semaphore = ref, semaphore("recv")

        def wait(self):
            described(self.ref, self.ref, all_sent[0], self.semaphore, twin).wait_recv()

    class Sent:
        def __init__(self, ref):
            self.ref, self.semaphore = ref, semaphore("send")
            all_sent.append(self.semaphore)

        def wait(self):
            described(self.ref, self.ref, self.semaphore, recv_sem.at[0], twin).wait_send()

    all_sent = []

    def move(src, dst, device, sent, landing):
        return functools.partial(described, src, dst, sent.semaphore, landing.semaphore, device)

    def start(*moves):
        for m in moves:
            m().start()

    first, second = pl.ds(0, HALF), pl.ds(HALF, ROWS - HALF)

    def blocks(n):
        return tokb.at[pl.ds(0, n)]

    tokens_sent = Sent(blocks(15))
    z_in, near_in, across_in, far_in, last_in = (Landing(blocks(n)) for n in (1, 2, 1, 2, 1))
    twins_in = [Landing(blocks(n)) for n in (4, 3, 1)]

    def block(src, dst, device, landing, rows=slice(None)):
        return move(tokb.at[src, rows], tokb.at[dst, rows], device, tokens_sent, landing)

    t_z = block(OWN, ZED, z_near, z_in)
    t_right, t_left = block(OWN, LEFT, y_right, near_in), block(OWN, RIGHT, y_left, near_in)
    t_fwd_r = block(LEFT, ACROSS, y_right, across_in, first)
    t_fwd_l = block(RIGHT, ACROSS, y_left, across_in, second)
    t_zright, t_zleft = block(ZED, ZLEFT, y_right, far_in), block(ZED, ZRIGHT, y_left, far_in)
    t_zfwd_r = block(ZLEFT, ZACROSS, y_right, last_in, first)
    t_zfwd_l = block(ZRIGHT, ZACROSS, y_left, last_in, second)
    waves = {OWN: 0, ZED: 0, LEFT: 0, RIGHT: 0, ACROSS: 1, ZLEFT: 1, ZRIGHT: 1, ZACROSS: 2}
    twins = {s: block(s, s + 1, twin, twins_in[w]) for s, w in waves.items()}

    class GateUp:
        def __init__(self, p):
            e, n = PIECES[p]
            top, low = pl.ds(0, COL // 2), pl.ds(COL // 2, COL // 2)
            far = 1 - zh

            def shards(k):
                return wg.at[e, n, pl.ds(0, k)]

            self.sent, self.near_in = Sent(shards(7)), Landing(shards(2))
            if p in Z_FIRST:
                self.z_in, self.far_in = Landing(shards(1)), Landing(shards(2))
                self.rest_in = across_in = Landing(shards(2))
                z_in, last_in = self.z_in, self.rest_in
            elif p == Z_ACROSS:
                self.across_in, self.rest_in = Landing(shards(1)), Landing(shards(4))
                across_in = self.across_in
                z_in = self.far_in = last_in = self.rest_in
            else:
                self.across_in, self.far_in = Landing(shards(1)), Landing(shards(2))
                self.rest_in, across_in = Landing(shards(2)), self.across_in
                z_in = last_in = self.rest_in

            def same(device, z, xx, landing, rows=slice(None)):
                ref = wg.at[e, n, z * 4 + xx, rows]
                return move(ref, ref, device, self.sent, landing)

            self.right, self.left = same(x_right, zh, x, self.near_in), same(x_left, zh, x, self.near_in)
            self.fwd_r, self.fwd_l = same(x_right, zh, xl, across_in, top), same(x_left, zh, xr, across_in, low)
            self.z = same(z_far, zh, x, z_in)
            if p in X_FIRST:
                self.zl, self.zr = same(z_far, zh, xl, self.far_in), same(z_far, zh, xr, self.far_in)
            else:
                self.zright, self.zleft = same(x_right, far, x, self.far_in), same(x_left, far, x, self.far_in)
            if p == Z_ACROSS:
                self.za = same(z_far, zh, xa, last_in)
            else:
                self.zfwd_r, self.zfwd_l = same(x_right, far, xl, last_in, top), same(x_left, far, xr, last_in, low)

    class Down:
        def __init__(self, half):
            top, low = pl.ds(0, FF // 2), pl.ds(FF // 2, FF // 2)
            cols = pl.ds(half * STEP, STEP)

            def slots(k):
                return wd.at[pl.ds(0, k), :, :, cols]

            self.sent = Sent(slots(7))
            self.near_in, self.across_in, self.z_in, self.far_in, self.last_in = (
                Landing(slots(k)) for k in (2, 1, 1, 2, 1)
            )

            def to(device, src, dst, landing, rows=slice(None)):
                return move(wd.at[src, :, rows, cols], wd.at[dst, :, rows, cols], device, self.sent, landing)

            self.right, self.left = to(x_right, 0, 1, self.near_in), to(x_left, 0, 3, self.near_in)
            self.z = to(z_far, 0, 4, self.z_in)
            self.fwd_r, self.fwd_l = to(x_right, 1, 2, self.across_in, top), to(x_left, 3, 2, self.across_in, low)
            self.zright, self.zleft = to(x_right, 4, 5, self.far_in), to(x_left, 4, 7, self.far_in)
            if half in Z_LAST:
                self.za = to(z_far, 2, 6, self.last_in)
            else:
                self.zfwd_r, self.zfwd_l = to(x_right, 5, 6, self.last_in, top), to(x_left, 7, 6, self.last_in, low)

    gu = [GateUp(p) for p in range(6)]
    dn = [Down(0), Down(1)]

    mine = zh * 4 + x
    def load(src, dst, name):
        pltpu.make_async_copy(src, dst, local_sem.at[name]).start()

    def loaded(dst, name):
        pltpu.make_async_copy(dst, dst, local_sem.at[name]).wait()

    def load_piece(p):
        e, n = PIECES[p]
        load(wgu.at[e, :, pl.ds(n * COL, COL)], wg.at[e, n, mine, :, pl.ds(0, COL)], p)
        load(wgu.at[e, :, pl.ds(FF + n * COL, COL)], wg.at[e, n, mine, :, pl.ds(COL, COL)], p)

    load_piece(4)
    load_piece(5)
    load(tok, tokb.at[OWN, pl.ds(0, TOK)], 6)
    for p in Z_FIRST:
        load_piece(p)
    load(wdn, wd.at[0], 7)

    barrier = pltpu.get_barrier_semaphore()
    for peer in (x_right, x_left, z_far, y_right, y_left, z_near, twin):
        pl.semaphore_signal(barrier, inc=1, device_id=peer, device_id_type=MESH)

    weights = probs[...] / jnp.sum(probs[...], axis=0, keepdims=True)
    high = weights.astype(BF16)
    middle = (weights - high.astype(F32)).astype(BF16)
    low = (weights - high.astype(F32) - middle.astype(F32)).astype(BF16)
    numbers = ids[...].astype(F32).astype(BF16)
    for k in range(TOP):
        parts = [v[k : k + 1, :] for v in (numbers, high, middle, low)]
        rows = jnp.concatenate([*parts, jnp.zeros((META - 4, TOK), BF16)], axis=0)
        tokb[OWN, TOK:ROWS, k * TOK : (k + 1) * TOK] = rows

    before = lax.broadcasted_iota(jnp.int32, (TOK, TOK), 0)
    after = lax.broadcasted_iota(jnp.int32, (TOK, TOK), 1)
    tri[...] = jnp.where(before < after, 1.0, 0.0).astype(BF16)
    pl.semaphore_wait(barrier, 7)

    slot_number = lax.broadcasted_iota(jnp.int32, (CAP, TOK), 0).astype(F32)

    def dispatch(r, carry):
        routing = tokb[r, pl.ds(TOK, META), :].astype(F32)
        places, shares = [], []
        for e in range(2):
            number = (ex * 2 + e).astype(F32)
            named = jnp.zeros((1, TOK), F32)
            weight = jnp.zeros((1, TOK), F32)
            for k in range(TOP):
                cols = slice(k * TOK, (k + 1) * TOK)
                hit = routing[0:1, cols] == number
                value = routing[1:2, cols] + routing[2:3, cols] + routing[3:4, cols]
                named = named + jnp.where(hit, 1.0, 0.0)
                weight = weight + jnp.where(hit, value, 0.0)
            many = jnp.broadcast_to(named, (16, TOK)).astype(BF16)
            slot = jnp.dot(many, tri[...], preferred_element_type=F32)[0:1, :]
            place = jnp.where(slot_number == slot, jnp.broadcast_to(named, (CAP, TOK)), 0.0)
            places.append(place)
            shares.append(place * weight)
        share = jnp.concatenate(shares, axis=0)
        upper = share.astype(BF16).astype(F32)
        pt[r, :, :] = jnp.concatenate([upper, share - upper], axis=0).T.astype(BF16)
        place = jnp.concatenate(places, axis=0).astype(BF16)
        rows = pl.ds(pl.multiple_of(r * CAP, CAP), CAP)
        for c in range(4):
            cols = slice(c * 512, (c + 1) * 512)
            picked = jnp.dot(place, tokb[r, 0:TOK, cols], preferred_element_type=F32).astype(BF16)
            xs[0, rows, cols] = picked[0:CAP]
            xs[1, rows, cols] = picked[CAP:]
        return carry

    def gate_up(p, *halves):
        e, n = PIECES[p]

        def tile(i, carry):
            rows = pl.ds(pl.multiple_of(i * 640, 640), 640)
            both = jnp.dot(xs[e, rows, :], wg[e, n].reshape(D, 2 * COL), preferred_element_type=F32)
            gate, up = both[:, :COL], both[:, COL:]
            hid[e, rows, n * COL : (n + 1) * COL] = (gate / (1.0 + jnp.exp(-gate)) * up).astype(BF16)
            return carry

        lax.fori_loop(halves[0], halves[-1] + 1, tile, 0)

    def gate_up_part(p, z, rows):
        e, n = PIECES[p]
        width = pl.ds(pl.multiple_of(z * (D // 2), D // 2), D // 2)
        return jnp.dot(
            xs[e, rows, width], wg[e, n, pl.ds(z * 4, 4)].reshape(D // 2, 2 * COL), preferred_element_type=F32
        )

    def gate_up_near(p, half):
        rows = pl.ds(half * 640, 640)
        part[rows, :] = gate_up_part(p, zh, rows)

    def gate_up_far(p):
        e, n = PIECES[p]

        def tile(i, carry):
            rows = pl.ds(pl.multiple_of(i * 640, 640), 640)
            both = part[rows, :] + gate_up_part(p, 1 - zh, rows)
            gate, up = both[:, :COL], both[:, COL:]
            hid[e, rows, n * COL : (n + 1) * COL] = (gate / (1.0 + jnp.exp(-gate)) * up).astype(BF16)
            return carry

        lax.fori_loop(0, 2, tile, 0)

    def own_piece(p):
        e, n = PIECES[p]
        loaded(wg.at[e, n, mine], p)
        start(gu[p].right, gu[p].left)

    def forward(p):
        gu[p].near_in.wait()
        start(gu[p].fwd_r, gu[p].fwd_l)

    def far_start(p):
        gu[p].z_in.wait()
        start(gu[p].zright, gu[p].zleft)

    def far_forward(p):
        gu[p].far_in.wait()
        start(gu[p].zfwd_r, gu[p].zfwd_l)

    own_piece(4)
    loaded(tokb.at[OWN, pl.ds(0, TOK)], 6)
    start(t_z, t_right, t_left, twins[OWN])
    own_piece(5)
    for p in Z_FIRST:
        own_piece(p)
    start(gu[0].z, gu[1].z, gu[4].z)

    forward(4)
    start(gu[4].zl, gu[4].zr, gu[2].z)
    forward(5)
    forward(0)
    near_in.wait()
    start(t_fwd_r, t_fwd_l)
    z_in.wait()
    start(t_zright, t_zleft, twins[ZED], twins[LEFT], twins[RIGHT])
    forward(1)
    forward(2)
    far_start(0)
    forward(3)
    twins_in[0].wait()
    lax.fori_loop(0, 8, dispatch, 0)
    gu[4].across_in.wait()
    start(gu[4].za, gu[3].z, gu[5].z, gu[5].zl, gu[5].zr)
    far_start(1)
    across_in.wait()
    start(twins[ACROSS])
    gu[5].across_in.wait()
    gate_up_near(5, 0)
    far_forward(0)
    far_start(2)
    far_in.wait()
    start(t_zfwd_r, t_zfwd_l, twins[ZLEFT], twins[ZRIGHT])
    far_forward(1)
    gu[4].rest_in.wait()
    gate_up(4, 0)
    gu[0].rest_in.wait()
    gate_up(0, 0)
    far_start(3)
    twins_in[1].wait()
    lax.fori_loop(8, 14, dispatch, 0)
    far_forward(2)
    last_in.wait()
    start(twins[ZACROSS])
    gu[1].rest_in.wait()
    gate_up(1, 0)
    twins_in[2].wait()
    lax.fori_loop(14, SRC, dispatch, 0)
    gate_up(4, 1)
    far_forward(3)
    gate_up(0, 1)
    tokens_sent.wait()
    for peer in (y_right, y_left, z_near, twin):
        pl.semaphore_signal(free_sem, inc=1, device_id=peer, device_id_type=MESH)
    loaded(wd.at[0], 7)
    start(dn[0].z, dn[1].z)
    gate_up(1, 1)
    gu[2].rest_in.wait()
    gate_up(2, 0, 1)
    far_forward(5)
    start(dn[0].right, dn[0].left, dn[1].right, dn[1].left)
    gate_up_near(5, 1)
    gu[3].rest_in.wait()
    gate_up(3, 0, 1)
    gu[5].rest_in.wait()
    gate_up_far(5)
    pl.semaphore_wait(free_sem, 4)

    upper, lower = pl.ds(0, TOK // 2), pl.ds(TOK // 2, TOK // 2)
    every = pl.ds(0, TOK)

    class Return:
        def __init__(self, n, slot, half):
            self.n, self.slot, self.half, self.z_first = n, slot, half, n in RETURN_Z_FIRST
            self.width = width = STEP if self.z_first else 2 * STEP
            pair, self.base = n // 2, n % 2 * 8 * STEP
            self.e, self.row = (0, pair * TOK) if pair < 5 else (1, (pair - 3) * TOK)
            self.twin_row = pair % 2 * TOK
            lane = pl.ds(pair % 4 * 512 + n % 2 * 256, width)

            def mine(col, cols, first=0, rows=TOK):
                return xs.at[self.e, pl.ds(self.row + first, rows), pl.ds(self.base + col, cols)]

            if self.z_first:
                self.z_lands = zbuf.at[RETURN_Z_FIRST.index(n)]
                z = (mine(4 * STEP, 4 * STEP), self.z_lands, z_near)
            else:
                z = (mine(STEP, STEP), tokb.at[14, every, pl.ds(n * STEP, STEP)], z_near)
            rows = TOK // 2
            self.twin_lands = tokb.at[pair, every, pl.ds(self.base, 8 * STEP)]
            theirs = xs.at[1, pl.ds(self.twin_row, TOK), pl.ds(self.base, 8 * STEP)]
            self.moves = dict(
                twin=(theirs, self.twin_lands, twin),
                right1=(mine(2 * width, width, 0, rows), tokb.at[8 + n // 8, upper, lane], y_right),
                left1=(mine(2 * width, width, rows, rows), tokb.at[8 + n // 8, lower, lane], y_left),
                right2=(mine(width, width), tokb.at[10 + n // 8, every, lane], y_right),
                left2=(mine(3 * width, width), tokb.at[12 + n // 8, every, lane], y_left),
                z=z,
            )
            self.ring = sums_sent
            self.twin_in, self.hop_in = Landing(self.twin_lands), Landing(tokb.at[8, every, pl.ds(0, width)])
            self.home_in = Landing(tokb.at[10, every, pl.ds(0, 2 * width)])
            self.z_in = Landing(z[1])
            self.landings = dict(
                twin=self.twin_in, right1=self.hop_in, left1=self.hop_in, right2=self.home_in, left2=self.home_in, z=self.z_in
            )
            column = (((zh + slot // 4) % 2) * 4 + (x + 4 - slot % 4) % 4) * COL + half * STEP
            self.store = pltpu.make_async_copy(
                ob.at[n], out.at[:, pl.ds(pl.multiple_of(column, STEP), STEP)], out_sem
            )

        def start(self, *names):
            for name in names:
                src, dst, device = self.moves[name]
                sent = twins_sent[self.n % 4] if name == "twin" else sums_sent
                start(move(src, dst, device, sent, self.landings[name]))

        def landed(self, name):
            return self.moves[name][1][...].astype(F32)

        def sums(self, col, cols, first=0, rows=TOK):
            return xs[self.e, self.row + first : self.row + first + rows, self.base + col : self.base + col + cols].astype(F32)

        def keep(self, total, col, first=0):
            rows, cols = total.shape
            at = slice(self.row + first, self.row + first + rows)
            xs[self.e, at, self.base + col : self.base + col + cols] = total.astype(BF16)

        def add(self, theirs, cols):
            def some(i, carry):
                at = pl.ds(pl.multiple_of(self.row + i * 64, 64), 64)
                got = theirs[pl.ds(pl.multiple_of(i * 64, 64), 64), :].astype(F32)
                lanes = slice(self.base, self.base + cols)
                xs[self.e, at, lanes] = (xs[self.e, at, lanes].astype(F32) + got).astype(BF16)
                return carry

            lax.fori_loop(0, TOK // 64, some, 0)

        def join_twin(self):
            self.twin_in.wait()
            self.add(self.twin_lands, 8 * STEP)
            self.start(*(("z",) if self.z_first else ("right1", "left1")))

        def second(self):
            width, rows = self.width, TOK // 2
            self.hop_in.wait()
            for there, col, first in (("right", width, 0), ("left", 3 * width, rows)):
                self.keep(self.sums(col, width, first, rows) + self.landed(there + "1"), col, first)
                self.start(there + "2")

        def home(self):
            self.home_in.wait()
            return self.sums(0, self.width) + self.landed("right2") + self.landed("left2")

        def hop(self):
            if self.z_first:
                self.z_in.wait()
                self.add(self.z_lands, 4 * STEP)
                self.start("right1", "left1")
            else:
                self.second()

        def third(self):
            if self.z_first:
                self.second()
            else:
                self.keep(self.home(), 0)
                self.start("z")

        def last(self):
            if self.z_first:
                total = self.home()
            else:
                self.z_in.wait()
                total = self.sums(0, STEP) + self.landed("z")
            ob[self.n] = total.astype(BF16)
            self.store.start()

    sums_sent = Sent(xs.at[:, pl.ds(0, STEPS * TOK // 4), pl.ds(0, 14 * STEP)])
    twins_sent = [Sent(xs.at[1, pl.ds(0, TOK), pl.ds(0, 8 * STEP)]) for _ in range(4)]
    returns, unit_steps = [], []
    for unit in UNITS:
        unit_steps.append([Return(len(returns) + i, slot, half) for i, (slot, half) in enumerate(unit)])
        returns += unit_steps[-1]

    def combine(steps):
        cols = len(steps) * STEP

        def side(mine, carry):
            def where(step):
                row = (1 - mine) * step.twin_row + mine * step.row
                return (1 - mine) + mine * step.e, pl.ds(pl.multiple_of(row, TOK), TOK)

            for (yy, zz), s in RETURN.items():
                r = s + 1 - mine
                total = jnp.dot(pt[r], yb[r, :, 0:cols], preferred_element_type=F32).astype(BF16)
                for i, step in enumerate(steps):
                    place = 4 * zz + yy if step.z_first else 2 * yy + zz
                    e, rows = where(step)
                    at = slice(step.base + place * STEP, step.base + (place + 1) * STEP)
                    xs[e, rows, at] = total[:, i * STEP : (i + 1) * STEP]

            @pl.when(mine == 0)
            def _():
                for step in steps:
                    step.start("twin")

            return carry

        lax.fori_loop(0, 2, side, 0)

    def compute(u):
        steps, unit = unit_steps[u], UNITS[u]
        for step in steps:
            if step.n >= 4:
                twins_sent[step.n % 4].wait()
        for slot, half in unit:
            if slot in (1, 3):
                once("n", half)
            elif slot == 2:
                once("a", half)
            elif slot == 4:
                once("f", half)
            elif slot in (5, 7):
                once("w", half)
            elif slot == 6:
                once("A", half)
        for e in range(2):
            shard = jnp.concatenate([wd[slot, e, :, half * STEP : (half + 1) * STEP] for slot, half in unit], axis=1)
            y_e = jnp.dot(hid[e], shard, preferred_element_type=F32).astype(BF16)
            for part_at in (0, 2 * CAP):
                rows = slice(part_at + e * CAP, part_at + (e + 1) * CAP)
                yb[:, rows, 0 : len(unit) * STEP] = y_e.reshape(SRC, CAP, -1)
        combine(steps)

    made = set()

    def once(what, half):
        if (what, half) in made:
            return
        made.add((what, half))
        d = dn[half]
        if what == "n":
            d.near_in.wait()
            start(d.fwd_r, d.fwd_l)
        elif what == "a":
            once("n", half)
            d.across_in.wait()
        elif what == "f":
            d.z_in.wait()
            start(d.zright, d.zleft)
        elif what == "w":
            once("f", half)
            d.far_in.wait()
        elif what == "F":
            once("w", half)
            start(d.zfwd_r, d.zfwd_l)
        elif what == "g":
            once("a", half)
            start(d.za)
        elif what == "A":
            once("g" if half in Z_LAST else "F", half)
            d.last_in.wait()

    do = {
        "C": compute, "T": lambda n: returns[n].join_twin(), "S": lambda n: returns[n].hop(),
        "H": lambda n: returns[n].third(), "L": lambda n: returns[n].last(),
        **{what: functools.partial(once, what) for what in "nfFg"},
    }
    for what, n in PLAN:
        do[what](n)
    sums_sent.wait()
    for n in range(STEPS - 4, STEPS):
        twins_sent[n % 4].wait()
    pltpu.make_async_copy(ob, ob, out_sem).wait()
    for group in (*gu, *dn):
        group.sent.wait()


def shards(tokens, expert_ids, route_probs, w_gate_up, w_down):
    any_spec = pl.BlockSpec(memory_space=pl.ANY)
    vmem_spec = pl.BlockSpec(memory_space=pltpu.VMEM)
    return pl.pallas_call(
        kernel,
        out_shape=jax.ShapeDtypeStruct((TOK, D), BF16),
        in_specs=[any_spec, vmem_spec, vmem_spec, any_spec, any_spec],
        out_specs=any_spec,
        scratch_shapes=[
            pltpu.VMEM((SRC, ROWS, D), BF16),
            pltpu.VMEM((2, 3, SHARDS, COL, 2 * COL), BF16),
            pltpu.VMEM((SHARDS, 2, FF, COL), BF16),
            pltpu.VMEM((2, SRC * CAP, D), BF16),
            pltpu.VMEM((2, SRC * CAP, FF), BF16),
            pltpu.VMEM((SRC, TOK, 4 * CAP), BF16),
            pltpu.VMEM((SRC, 4 * CAP, COL), BF16),
            pltpu.VMEM((TOK, TOK), BF16),
            pltpu.VMEM((len(RETURN_Z_FIRST), TOK, 4 * STEP), BF16),
            pltpu.VMEM((STEPS, TOK, STEP), BF16),
            pltpu.VMEM((SRC * CAP, 2 * COL), F32),
            pltpu.SemaphoreType.DMA((8,)),
            pltpu.SemaphoreType.DMA((SENDS,)),
            pltpu.SemaphoreType.DMA((LANDINGS,)),
            pltpu.SemaphoreType.DMA,
            pltpu.SemaphoreType.REGULAR,
        ],
        compiler_params=pltpu.CompilerParams(
            collective_id=0, has_side_effects=True, vmem_limit_bytes=67_000_000
        ),
    )(tokens, expert_ids.T, route_probs.T, w_gate_up, w_down)


def solution(mesh):
    spec = P(("dp", "expert"), None)
    in_specs = (spec, spec, spec, P("expert", "dp", None), P("expert", None, "dp"))
    return jax.shard_map(shards, mesh=mesh, in_specs=in_specs, out_specs=spec, check_vma=False)
```

time: 184 us -> 178 us (0.967)
  Pallas kernels: 182 us -> 176 us
    pallas_call x1, Pallas kernels: 182 us -> 176 us  [shards(): pl.pallas_call(kernel, out_shape=jax.ShapeDtypeStruct((TOK, D), BF16), in...]
where the time goes in v3:
time: 178 us
  Pallas kernels  176 us (99%)
  local copies, waits for them, and re-layouts  2.3 us (1%)
    pallas_call x1, Pallas kernels, shards(): pl.pallas_call(kernel, out_shape=jax.ShapeDtypeStruct((TOK, D), BF16), in...  176 us

profile of v3, /device:TPU:0, one launch (start us, length us, event | category | flops | bytes accessed | tf_op | source)
XLA Modules:
  0.0 177.9 jit_solution(14890860047965444080)
XLA Ops:
  0.0 175.6 %shard_map.55 = bf16[256,2048]{1,0:T(8,128)(2,1)} custom-call(bf16[256,2048]{1,0:T(8,128)(2,1)} %tok.1, s32[8,256]{1,0:T(8,128)} %bitcast.2, f32[8,256]{1,0:T(8,128)} %bitcast.3, bf16[2,256,1536]{2,1,0:T(8,128)(2,1)} %wgu.1, bf16[2,768,256]{2,1,0:T(8,128)(2,1)} %wdn.1), custom_call_target="tpu_custom_call" | custom-call | tf_op jit(solution)/shard_map/pallas_call | solution.py:605
  175.6 2.3 %copy.7 = bf16[256,2048]{1,0:T(8,128)(2,1)} copy(bf16[256,2048]{1,0:T(8,128)(2,1)} %shard_map.55) | data formatting | bytes 2097152

commit v4 on v3

--- a/solution.py
+++ b/solution.py
@@ -13,8 +13,9 @@
 
 TOK = 256
 META = 16
+META_COLS = 512
 ROWS = TOK + META
-HALF = 144
+HALF = TOK // 2
 D = 2048
 FF = 768
 TOP = 8
@@ -24,8 +25,8 @@
 SHARDS = 8
 STEPS = 16
 STEP = COL // 2
-LANDINGS = 8 + 4 * 4 + 3 + 4 + 2 * 5 + 16 * 4
-SENDS = 1 + 6 + 2 + 1 + 4
+LANDINGS = 2 * 8 + 4 * 4 + 3 + 4 + 2 * 5 + 16 * 4
+SENDS = 2 + 6 + 2 + 1 + 4
 
 OWN, ZED, LEFT, RIGHT, ACROSS, ZLEFT, ZRIGHT, ZACROSS = range(0, 16, 2)
 RETURN = {
@@ -107,19 +108,35 @@
 
     def start(*moves):
         for m in moves:
-            m().start()
-
-    first, second = pl.ds(0, HALF), pl.ds(HALF, ROWS - HALF)
+            for each in m if isinstance(m, tuple) else (m,):
+                each().start()
+
+    first, second = pl.ds(0, HALF), pl.ds(HALF, HALF)
+    body, routing_rows = (pl.ds(0, TOK),), (pl.ds(TOK, META), pl.ds(0, META_COLS))
 
     def blocks(n):
-        return tokb.at[pl.ds(0, n)]
-
-    tokens_sent = Sent(blocks(15))
-    z_in, near_in, across_in, far_in, last_in = (Landing(blocks(n)) for n in (1, 2, 1, 2, 1))
-    twins_in = [Landing(blocks(n)) for n in (4, 3, 1)]
-
-    def block(src, dst, device, landing, rows=slice(None)):
-        return move(tokb.at[src, rows], tokb.at[dst, rows], device, tokens_sent, landing)
+        return tokb.at[(pl.ds(0, n), *body)], tokb.at[(pl.ds(0, n), *routing_rows)]
+
+    class Both:
+        def __init__(self, kind, n):
+            self.tokens, self.routing = (kind(ref) for ref in blocks(n))
+
+        def wait(self):
+            self.tokens.wait()
+            self.routing.wait()
+
+    tokens_sent = Both(Sent, 15)
+    z_in, near_in, across_in, far_in, last_in = (Both(Landing, n) for n in (1, 2, 1, 2, 1))
+    twins_in = [Both(Landing, n) for n in (4, 3, 1)]
+
+    def block(src, dst, device, landing, rows=None):
+        routing = move(
+            tokb.at[(src, *routing_rows)], tokb.at[(dst, *routing_rows)], device, tokens_sent.routing, landing.routing
+        )
+        if rows is None:
+            rows = pl.ds(0, TOK)
+        tokens = move(tokb.at[src, rows], tokb.at[dst, rows], device, tokens_sent.tokens, landing.tokens)
+        return (tokens,) if rows is second else (routing, tokens)
 
     t_z = block(OWN, ZED, z_near, z_in)
     t_right, t_left = block(OWN, LEFT, y_right, near_in), block(OWN, RIGHT, y_left, near_in)
@@ -226,10 +243,9 @@
     middle = (weights - high.astype(F32)).astype(BF16)
     low = (weights - high.astype(F32) - middle.astype(F32)).astype(BF16)
     numbers = ids[...].astype(F32).astype(BF16)
-    for k in range(TOP):
-        parts = [v[k : k + 1, :] for v in (numbers, high, middle, low)]
-        rows = jnp.concatenate([*parts, jnp.zeros((META - 4, TOK), BF16)], axis=0)
-        tokb[OWN, TOK:ROWS, k * TOK : (k + 1) * TOK] = rows
+    for lane in range(2):
+        rows = [v[k : k + 1, :] for v in (numbers, high, middle, low) for k in range(lane, TOP, 2)]
+        tokb[OWN, TOK:ROWS, lane * TOK : (lane + 1) * TOK] = jnp.concatenate(rows, axis=0)
 
     before = lax.broadcasted_iota(jnp.int32, (TOK, TOK), 0)
     after = lax.broadcasted_iota(jnp.int32, (TOK, TOK), 1)
@@ -239,16 +255,17 @@
     slot_number = lax.broadcasted_iota(jnp.int32, (CAP, TOK), 0).astype(F32)
 
     def dispatch(r, carry):
-        routing = tokb[r, pl.ds(TOK, META), :].astype(F32)
+        routing = tokb[r, pl.ds(TOK, META), pl.ds(0, META_COLS)].astype(F32)
         places, shares = [], []
         for e in range(2):
             number = (ex * 2 + e).astype(F32)
             named = jnp.zeros((1, TOK), F32)
             weight = jnp.zeros((1, TOK), F32)
             for k in range(TOP):
-                cols = slice(k * TOK, (k + 1) * TOK)
-                hit = routing[0:1, cols] == number
-                value = routing[1:2, cols] + routing[2:3, cols] + routing[3:4, cols]
+                cols = slice(k % 2 * TOK, (k % 2 + 1) * TOK)
+                mark, high, middle, low = (routing[4 * i + k // 2 : 4 * i + k // 2 + 1, cols] for i in range(4))
+                hit = mark == number
+                value = high + middle + low
                 named = named + jnp.where(hit, 1.0, 0.0)
                 weight = weight + jnp.where(hit, value, 0.0)
             many = jnp.broadcast_to(named, (16, TOK)).astype(BF16)

time: 178 us -> 177 us (level)
  no operation moved by 1% of the time
where the time goes in v4:
time: 177 us
  Pallas kernels  175 us (99%)
  local copies, waits for them, and re-layouts  2.3 us (1%)
    pallas_call x1, Pallas kernels, shards(): pl.pallas_call(kernel, out_shape=jax.ShapeDtypeStruct((TOK, D), BF16), in...  175 us

profile of v4, /device:TPU:0, one launch (start us, length us, event | category | flops | bytes accessed | tf_op | source)
XLA Modules:
  0.0 177.0 jit_solution(5160256340090147201)
XLA Ops:
  0.0 174.6 %shard_map.55 = bf16[256,2048]{1,0:T(8,128)(2,1)} custom-call(bf16[256,2048]{1,0:T(8,128)(2,1)} %tok.1, s32[8,256]{1,0:T(8,128)} %bitcast.2, f32[8,256]{1,0:T(8,128)} %bitcast.3, bf16[2,256,1536]{2,1,0:T(8,128)(2,1)} %wgu.1, bf16[2,768,256]{2,1,0:T(8,128)(2,1)} %wdn.1), custom_call_target="tpu_custom_call" | custom-call | tf_op jit(solution)/shard_map/pallas_call | solution.py:622
  174.7 2.3 %copy.7 = bf16[256,2048]{1,0:T(8,128)(2,1)} copy(bf16[256,2048]{1,0:T(8,128)(2,1)} %shard_map.55) | data formatting | bytes 2097152

commit v5 on v4

--- a/solution.py
+++ b/solution.py
@@ -25,7 +25,7 @@
 SHARDS = 8
 STEPS = 16
 STEP = COL // 2
-LANDINGS = 2 * 8 + 4 * 4 + 3 + 4 + 2 * 5 + 16 * 4
+LANDINGS = 2 * 8 + 4 * 4 + 3 + 3 + 2 * 5 + 16 * 4
 SENDS = 2 + 6 + 2 + 1 + 4
 
 OWN, ZED, LEFT, RIGHT, ACROSS, ZLEFT, ZRIGHT, ZACROSS = range(0, 16, 2)
@@ -162,7 +162,7 @@
                 self.z_in, self.far_in = Landing(shards(1)), Landing(shards(2))
                 self.rest_in = across_in = Landing(shards(2))
                 z_in, last_in = self.z_in, self.rest_in
-            elif p == Z_ACROSS:
+            elif p in X_FIRST:
                 self.across_in, self.rest_in = Landing(shards(1)), Landing(shards(4))
                 across_in = self.across_in
                 z_in = self.far_in = last_in = self.rest_in
@@ -182,7 +182,7 @@
                 self.zl, self.zr = same(z_far, zh, xl, self.far_in), same(z_far, zh, xr, self.far_in)
             else:
                 self.zright, self.zleft = same(x_right, far, x, self.far_in), same(x_left, far, x, self.far_in)
-            if p == Z_ACROSS:
+            if p in X_FIRST:
                 self.za = same(z_far, zh, xa, last_in)
             else:
                 self.zfwd_r, self.zfwd_l = same(x_right, far, xl, last_in, top), same(x_left, far, xr, last_in, low)
@@ -365,6 +365,7 @@
     across_in.wait()
     start(twins[ACROSS])
     gu[5].across_in.wait()
+    start(gu[5].za)
     gate_up_near(5, 0)
     far_forward(0)
     far_start(2)
@@ -396,7 +397,6 @@
     gate_up(1, 1)
     gu[2].rest_in.wait()
     gate_up(2, 0, 1)
-    far_forward(5)
     start(dn[0].right, dn[0].left, dn[1].right, dn[1].left)
     gate_up_near(5, 1)
     gu[3].rest_in.wait()

time: 177 us -> 176 us (level)
  no operation moved by 1% of the time
where the time goes in v5:
time: 176 us
  Pallas kernels  174 us (99%)
  local copies, waits for them, and re-layouts  2.3 us (1%)
    pallas_call x1, Pallas kernels, shards(): pl.pallas_call(kernel, out_shape=jax.ShapeDtypeStruct((TOK, D), BF16), in...  174 us

profile of v5, /device:TPU:0, one launch (start us, length us, event | category | flops | bytes accessed | tf_op | source)
XLA Modules:
  0.0 176.3 jit_solution(14875599896832441769)
XLA Ops:
  0.0 173.9 %shard_map.55 = bf16[256,2048]{1,0:T(8,128)(2,1)} custom-call(bf16[256,2048]{1,0:T(8,128)(2,1)} %tok.1, s32[8,256]{1,0:T(8,128)} %bitcast.2, f32[8,256]{1,0:T(8,128)} %bitcast.3, bf16[2,256,1536]{2,1,0:T(8,128)(2,1)} %wgu.1, bf16[2,768,256]{2,1,0:T(8,128)(2,1)} %wdn.1), custom_call_target="tpu_custom_call" | custom-call | tf_op jit(solution)/shard_map/pallas_call | solution.py:622
  174.0 2.3 %copy.7 = bf16[256,2048]{1,0:T(8,128)(2,1)} copy(bf16[256,2048]{1,0:T(8,128)(2,1)} %shard_map.55) | data formatting | bytes 2097152
